TPU v7x, 256 devices: a whole 4x4x8 slice. The times are simulated.
256 devices in a mesh: seq: 32 (over y, x, core), vocab: 8 (over z).
Axes of the slice: x: 4, y: 4, z: 8, core: 2. Of those that a mesh axis runs over, the one named last changes fastest.
Arguments:
- hidden: bfloat16 [3840, 4096], P('seq'), may hold values from -32 to 32
- head_weight: bfloat16 [4096, 98304], P(None, ('seq', 'vocab')), may hold values from -0.84375 to 0.84375
- labels: int32 [3840], P('seq'), may hold values from 0 to 98303
- lengths: int32 [32], replicated, may hold values from 1 to 120, 1920 in all
- pair_map: int32 [32], replicated, may hold values from 0 to 31, each once
- ref_margin: float32 [16], replicated, may hold values from -240 to 240
Outputs:
- seq_logps: float32 [32], replicated
- pair_loss: float32 [16], replicated
- z_loss: float32 [], replicated
Inputs may be any that keep to these rules, and one draw needn't show every extreme that they name: The lengths sum to 1920 and the longest is exactly 120. Each response appears once; pair p compares response pair_map[2p], chosen, with response pair_map[2p+1], rejected.
All inputs are finite; a program needn't handle non-finite values.
Results may differ from a plain program's by a relative error of at most 0.0003.
Values may be sent and summed in bfloat16 or wider, within the bound.
A program may use at most 192 MiB of HBM per device.

v0:
```python
import jax
import jax.numpy as jnp
from jax import lax
from jax.sharding import Mesh
from jax.sharding import PartitionSpec as P

SEQ = ("seq_0", "seq_1", "seq_2")
SEQ_VOCAB = ("seq_0", "seq_1", "seq_2", "vocab")


pref_beta = 0.05
zloss_weight = 0.0001


def all_in_one(array, axis):
    leaves = jax.tree.leaves(array)
    turns = sorted(range(len(leaves)), key=lambda k: -leaves[k].size)
    width = (1, *leaves[turns[0]].shape)[-1]
    lines = [
        jnp.pad(leaves[k].reshape(-1), (0, -leaves[k].size % width)).reshape(-1, width)
        for k in turns
    ]
    both, at, found = (lax.all_gather(jnp.concatenate(lines), axis), 0, {})
    for k, line in zip(turns, lines):
        section = both[:, at : at + len(line)].reshape(len(both), -1)
        found[k] = section[:, : leaves[k].size].reshape(-1, *leaves[k].shape)
        at += len(line)
    numbers = iter(range(len(leaves)))
    return jax.tree.map(lambda _: found[next(numbers)], array)


def combined_by_axis(array, axes, combine):
    for axis in axes:
        pieces = all_in_one(array, axis)
        array = jax.tree.map(lambda part: part[0], pieces)
        for k in range(1, lax.axis_size(axis)):
            array = combine(array, jax.tree.map(lambda part: part[k], pieces))
    return array


def per_device(hidden, head_weight, labels, lengths, pair_map, ref_margin):
    vocab_devices = lax.axis_size("vocab")
    shard_rows = hidden.shape[0]
    columns = head_weight.shape[1]
    seq_total = lengths.shape[0]
    col_first = (lax.axis_index(SEQ) * vocab_devices + lax.axis_index("vocab")) * columns
    col_ids = col_first + jnp.arange(columns, dtype=jnp.int32)
    seq_ids = jnp.arange(seq_total, dtype=jnp.int32)
    logits = jnp.dot(
        lax.all_gather(hidden, SEQ, axis=0, tiled=True),
        head_weight,
        preferred_element_type=jnp.float32,
    )
    local_max = jnp.max(logits, axis=1)
    local_sum = jnp.sum(jnp.exp(logits - local_max[:, None]), axis=1)
    picked = jnp.sum(
        jnp.where(
            lax.all_gather(labels, SEQ, axis=0, tiled=True)[:, None] == col_ids[None, :],
            logits,
            0.0,
        ),
        axis=1,
    )
    fresh = (local_max, local_sum, picked)
    local_max, local_sum, picked = tuple((fresh_part for fresh_part in fresh))

    def combine(first_part, second_part):
        highest = jnp.maximum(first_part[0], second_part[0])
        summed = first_part[1] * jnp.exp(first_part[0] - highest) + second_part[1] * jnp.exp(
            second_part[0] - highest
        )
        return (highest, summed, first_part[2] + second_part[2])

    top_score, exp_total, label_logit = combined_by_axis(
        (local_max, local_sum, picked), SEQ_VOCAB, combine
    )
    log_norm = (top_score + jnp.log(exp_total)).reshape(seq_total, shard_rows)
    label_logit = label_logit.reshape(seq_total, shard_rows)
    live_mask = jnp.arange(shard_rows, dtype=jnp.int32)[None, :] < lengths[:, None]
    seq_logps = jnp.sum(jnp.where(live_mask, label_logit - log_norm, 0.0), axis=1)
    select = (pair_map[:, None] == seq_ids[None, :]).astype(jnp.float32)
    ordered = jnp.dot(select, seq_logps, precision=lax.Precision.HIGHEST).reshape(seq_total // 2, 2)
    pair_loss = jax.nn.softplus(-pref_beta * (ordered[:, 0] - ordered[:, 1] - ref_margin))
    live_count = jnp.sum(live_mask.astype(jnp.float32))
    z_loss = zloss_weight * jnp.sum(jnp.where(live_mask, log_norm * log_norm, 0.0)) / live_count
    return (seq_logps, pair_loss, z_loss)


def solution(mesh):
    torus = Mesh(
        mesh.devices.reshape(4, 4, 2, mesh.shape["vocab"]), ("seq_0", "seq_1", "seq_2", "vocab")
    )
    return jax.shard_map(
        per_device,
        mesh=torus,
        in_specs=(P(SEQ, None), P(None, SEQ_VOCAB), P(SEQ), P(), P(), P()),
        out_specs=(P(), P(), P()),
        check_vma=False,
    )
```

profile of v0, /device:TPU:1, one launch (start us, length us, event | category | flops | bytes accessed | tf_op | source)
XLA Modules:
  0.0 235.2 jit_solution(9365417686779292832)
XLA Ops:
  7.2 0.7 all-gather.10.cloned.1.call-update
  7.9 0.9 iota_compare_fusion.1
  8.8 0.1 lt.30
  9.0 0.7 eq.32
  9.7 1.3 dynamic-slice
  11.6 0.9 dynamic-update-slice
  12.5 128.0 %all-reduce = s32[3840]{0:T(1024)S(1)} all-reduce(s32[3840]{0:T(1024)S(1)} %dynamic-update-slice), channel_id=1, replica_groups=mesh['seq_0'=4,'seq_1'=4,'seq_2'=2,'vocab'=8] {'seq_0','seq_1','seq_2'}, use_global_device_ids=true, to_apply=%add | all-reduce | flops 3840 | bytes 30720
  140.5 0.1 iota_compare_fusion
  140.7 19.4 %fusion.67 = (f32[3840]{0:T(1024)S(1)}, f32[3840,384]{0,1:T(8,128)}) fusion(bf16[3840,4096]{1,0:T(8,128)(2,1)} %all-gather.10.cloned.1.call-done, bf16[4096,384]{1,0:T(8,128)(2,1)S(1)} %copy-done), kind=kOutput, calls=%fused_computation.142 | convolution fusion | flops 12081065984 | bytes 40516608 | tf_op jit(solution)/shard_map/dot_general | solution.py:49
  160.1 3.5 %exponential_reduce_fusion = (f32[3840]{0:T(1024)S(1)}, f32[3840]{0:T(1024)S(1)}) fusion(f32[3840,384]{0,1:T(8,128)} %get-tuple-element.32, f32[3840]{0:T(1024)S(1)} %get-tuple-element.31, s32[384]{0:T(512)S(1)} %iota_add_fusion, s32[3840]{0:T(1024)S(1)} %all-reduce), kind=kLoop, calls=%fused_computation.1 | loop fusion | flops 7365120 | bytes 5961216 | tf_op jit(solution)/shard_map/reduce_sum | solution.py:55
  163.7 9.3 %all-gather.4 = f32[4,3,3840]{2,1,0:T(4,128)S(1)} all-gather(f32[1,3,3840]{2,1,0:T(4,128)S(1)} %maximum_bitcast_fusion), channel_id=2, replica_groups=mesh['seq_0'=4,'seq_1'=4,'seq_2'=2,'vocab'=8] {'seq_0'}, dimensions={0}, use_global_device_ids=true | all-gather | bytes 230400 | tf_op jit(solution)/shard_map/all_gather | solution.py:23
  173.1 0.2 fusion.33
  173.3 9.3 %all-gather.5 = f32[4,3,3840]{2,1,0:T(4,128)S(1)} all-gather(f32[1,3,3840]{2,1,0:T(4,128)S(1)} %maximum_bitcast_fusion.1), channel_id=3, replica_groups=mesh['seq_0'=4,'seq_1'=4,'seq_2'=2,'vocab'=8] {'seq_1'}, dimensions={0}, use_global_device_ids=true | all-gather | bytes 230400 | tf_op jit(solution)/shard_map/all_gather | solution.py:23
  182.7 0.2 fusion.23
  182.9 13.0 %all-gather.6 = f32[2,3,3840]{2,1,0:T(4,128)S(1)} all-gather(f32[1,3,3840]{2,1,0:T(4,128)S(1)} %maximum_bitcast_fusion.2), channel_id=4, replica_groups=mesh['seq_0'=4,'seq_1'=4,'seq_2'=2,'vocab'=8] {'seq_2'}, dimensions={0}, use_global_device_ids=true | all-gather | bytes 138240 | tf_op jit(solution)/shard_map/all_gather | solution.py:23
  196.0 23.7 %all-gather.7 = f32[8,3,3840]{2,1,0:T(4,128)S(1)} all-gather(f32[1,3,3840]{2,1,0:T(4,128)S(1)} %maximum_bitcast_fusion.3), channel_id=5, replica_groups=mesh['seq_0'=4,'seq_1'=4,'seq_2'=2,'vocab'=8] {'vocab'}, dimensions={0}, use_global_device_ids=true | all-gather | bytes 414720 | tf_op jit(solution)/shard_map/all_gather | solution.py:23
  219.7 0.5 slice_reduce_fusion.7
  220.2 0.2 copy-done.1
  220.5 0.1 slice_reduce_fusion.6
  220.6 0.1 reshape.734
  220.7 0.1 squeeze.172
  220.8 2.3 select_reduce_fusion.2
  223.1 0.1 squeeze.171
  223.3 0.1 squeeze.170
  223.4 0.1 squeeze.162
  223.6 0.1 squeeze.161
  223.8 0.1 squeeze.160
  223.8 0.1 squeeze.167
  224.0 0.1 squeeze.166
  224.4 0.8 convert_reduce_fusion
  225.1 0.1 fusion.14
  225.3 0.6 compare_select_fusion
  (32 shorter events, 1.2 us)
Async XLA Ops:
  7.2 133.5 %copy-start = (bf16[4096,384]{1,0:T(8,128)(2,1)S(1)}, bf16[4096,384]{1,0:T(8,128)(2,1)}, u32[]{:S(2)}) copy-start(bf16[4096,384]{1,0:T(8,128)(2,1)} %param.7) | copy-start | bytes 9437188
  7.2 133.5 %all-gather.10.cloned.1.call-start = ((), (), s32[]{:S(2)}) async-start(), calls=%async_computation | async-start | bytes 32440320 | tf_op jit(solution)/shard_map/all_gather | solution.py:50
  160.1 64.3 %copy-start.2 = (s32[32]{0:T(128)S(1)}, s32[32]{0:T(128)}, u32[]{:S(2)}) copy-start(s32[32]{0:T(128)} %param.9) | copy-start | bytes 388
  160.1 65.2 %copy-start.4 = (f32[16]{0:T(128)S(1)}, f32[16]{0:T(128)}, u32[]{:S(2)}) copy-start(f32[16]{0:T(128)} %param.11) | copy-start | bytes 196
  219.7 0.8 copy-start.1
  225.1 2.1 copy-start.3
Sparse Core Ops, SparseCore 0:
  10.5 118.1 all-gather.9
where the time goes:
time: 239 us; the launch traced here: 235 us
  blocking collectives  183 us (77%)
  matrix products  19.5 us (8%)
  between operations  17.5 us (7%)
  other arithmetic  9.4 us (4%)
  local copies, waits for them, and re-layouts  4.77 us (2%)
    unnamed x1, blocking collectives  128 us
    all_gather x4, blocking collectives, all_in_one(): both, at, found = (lax.all_gather(jnp.concatenate(lines), axis), 0, {})  55.3 us
    dot_general x1, matrix products, per_device(): jnp.dot(lax.all_gather(hidden, SEQ, axis=0, tiled=True), head_weight, pre...  19.4 us
  transfers between devices with their start and end apart: 1, of which 0 were waited for; matrix products, arithmetic and copies ran while one was open for 2% of the time, Pallas kernels for 0%

commit v1 on v0

v1 whole, which is shorter than its diff:
```python
import functools
import heapq

import jax
import jax.numpy as jnp
from jax import lax
from jax.experimental import pallas as pl
from jax.experimental.pallas import tpu as pltpu
from jax.sharding import Mesh
from jax.sharding import PartitionSpec as P

SEQ = ("seq_0", "seq_1", "seq_2")
SEQ_VOCAB = ("seq_0", "seq_1", "seq_2", "vocab")
MESH = pl.DeviceIdType.MESH

pref_beta = 0.05
zloss_weight = 0.0001

LANES = 128
UNROLL = 4
BATCH = 8
FLIGHT = 2
WIRE = 1.32
HOP = 1.1


def broadcast_tree(dims):
    nodes = [
        (a, b, c)
        for a in range(dims[0])
        for b in range(dims[1])
        for c in range(dims[2])
        if (a, b, c) != (0, 0, 0)
    ]
    choices = {}
    for node in nodes:
        ways = []
        for axis in range(3):
            at, size = node[axis], dims[axis]
            if at and at <= size // 2:
                ways.append((axis, 1))
            if at and at >= size - size // 2:
                ways.append((axis, -1))
        choices[node] = ways
    load = {}
    taken = {}
    for node in sorted(nodes, key=lambda n: (len(choices[n]), n)):
        way = min(choices[node], key=lambda w: (load.get(w, 0), w))
        taken[node] = way
        load[way] = load.get(way, 0) + 1
    moved = True
    while moved:
        moved = False
        for node in nodes:
            for way in choices[node]:
                if load.get(way, 0) + 1 < load[taken[node]]:
                    load[taken[node]] -= 1
                    load[way] = load.get(way, 0) + 1
                    taken[node] = way
                    moved = True
    return taken


def before(node, way, dims):
    place = list(node)
    place[way[0]] = (place[way[0]] - way[1]) % dims[way[0]]
    return tuple(place)


def gather_plan(dims):
    taken = broadcast_tree(dims)
    children = {}
    for node, way in taken.items():
        children.setdefault(before(node, way, dims), []).append((node, way))

    @functools.cache
    def height(node):
        return max([1 + height(child) for child, _ in children.get(node, [])], default=0)

    @functools.cache
    def weight(node):
        return 1 + sum(weight(child) for child, _ in children.get(node, []))

    ways = sorted(set(taken.values()))
    ready = {way: [] for way in ways}
    free = {way: 0.0 for way in ways}
    flying = {way: 0 for way in ways}
    events = [(0.0, 0, "arrive", (0, 0, 0))]
    count = 1
    plan = []
    while events:
        now, _, kind, item = heapq.heappop(events)
        if kind == "arrive":
            plan.append(("wait", item, None, None))
            for child, way in children.get(item, []):
                ready[way].append(child)
        else:
            flying[item] -= 1
        for way in ways:
            while ready[way] and flying[way] < FLIGHT:
                ready[way].sort(key=lambda n: (-height(n), -weight(n), n))
                child = ready[way].pop(0)
                end = max(now, free[way]) + WIRE
                free[way] = end
                flying[way] += 1
                plan.append(("send", before(child, way, dims), child, way))
                heapq.heappush(events, (end, count, "sent", way))
                heapq.heappush(events, (end + HOP, count + 1, "arrive", child))
                count += 2
    return plan


def log_one_plus(u):
    w = u / (2.0 + u)
    square = w * w
    total = jnp.full_like(w, 1.0 / 17.0)
    for odd in (15, 13, 11, 9, 7, 5, 3, 1):
        total = total * square + 1.0 / odd
    return 2.0 * w * total


def iota(shape, dim):
    return lax.broadcasted_iota(jnp.int32, shape, dim)


def scatter_scalars(ids, values):
    out = jnp.zeros(ids.shape, jnp.int32)
    for k, value in enumerate(values):
        out = jnp.where(ids == k, value, out)
    return out


def sums_before(ids, values):
    out = jnp.zeros(ids.shape, jnp.int32)
    for k, value in enumerate(values):
        out = out + jnp.where(ids > k, value, 0)
    return out


def kernel(
    dims,
    hidden_hbm,
    weight_hbm,
    labels_ref,
    lengths_ref,
    pairs_ref,
    margins_ref,
    out_ref,
    hidden,
    weight,
    parcels,
    received,
    label_row,
    labels_all,
    gathered,
    scores,
    label_place,
    stats,
    stats_in,
    merged,
    merged_in,
    sums,
    sums_in,
    load_sem,
    parcel_sem,
    label_sem,
    block_send,
    twin_send,
    block_recv,
    twin_recv,
    stat_sem,
    merged_sem,
    sums_sem,
):
    ny, nx, nz = dims
    plane = ny * nx
    seqs = lengths_ref.shape[0]
    pairs = margins_ref.shape[0]
    window = hidden.shape[0]
    slots = parcels.shape[1]
    rows = gathered.shape[2]
    columns = weight.shape[1]
    halves = plane // nz
    part_rows = rows // halves
    y, x = lax.axis_index("seq_0"), lax.axis_index("seq_1")
    core, z = lax.axis_index("seq_2"), lax.axis_index("vocab")
    here = y * nx + x
    mine = here * 2 + core
    twin = 1 - core

    def shifted(dy, dx, dz):
        return ((y + dy) % ny, (x + dx) % nx, (z + dz) % nz)

    def chip_of(node):
        cy, cx, cz = shifted(-node[0] + ny, -node[1] + nx, -node[2] + nz)
        return (cy * nx + cx) * nz + cz

    load_hidden = pltpu.make_async_copy(hidden_hbm, hidden, load_sem.at[0])
    load_weight = pltpu.make_async_copy(weight_hbm, weight, load_sem.at[1])
    load_hidden.start()
    load_weight.start()

    far = lambda n, size: min(n, size - n)
    plane_steps = sorted(
        [(a, b) for a in range(ny) for b in range(nx)],
        key=lambda s: -(far(s[0], ny) + far(s[1], nx)),
    )
    plane_peers = [(a, b, c) for a, b in plane_steps for c in (0, 1) if (a, b, c) != (0, 0, 0)]

    def peer_of(step):
        py, px, _ = shifted(step[0], step[1], 0)
        pc = twin if step[2] else core
        return py, px, pc

    barrier = pltpu.get_barrier_semaphore()
    for step in plane_peers:
        py, px, pc = peer_of(step)
        pl.semaphore_signal(barrier, inc=1, device_id=(py, px, pc, z), device_id_type=MESH)
    z_steps = sorted({1 % nz, nz - 1} - {0})
    for dz in z_steps:
        pl.semaphore_signal(
            barrier, inc=1, device_id=(y, x, core, (z + dz) % nz), device_id_type=MESH
        )

    lens = [lengths_ref[s] for s in range(seqs)]
    slot_ids = iota((1, seqs * slots), 1)
    slot_seq = slot_ids // slots
    first = sums_before(slot_seq, lens)
    place = nz * (slot_ids % slots) + ((z - first) & (nz - 1))
    row_of_slot = jnp.where(
        place < scatter_scalars(slot_seq, lens), (first + place - z) // nz, -1
    )
    own_first = jnp.int32(0)
    for s in range(seqs - 1):
        own_first = own_first + jnp.where(mine > s, lens[s], 0)
    own_place = nz * iota((slots, window), 0) + ((z - own_first) & (nz - 1))
    choose = jnp.where(own_place == iota((slots, window), 1), 1.0, 0.0).astype(jnp.bfloat16)

    label_row[...] = jnp.zeros(label_row.shape, jnp.int32)
    label_row[0:1, 0:window] = labels_ref[...]
    labels_all[mine] = label_row[...]
    scores[...] = jnp.zeros(scores.shape, jnp.float32)
    load_hidden.wait()
    chosen = jnp.dot(choose, hidden[...], preferred_element_type=jnp.float32)
    chosen = chosen.astype(jnp.bfloat16)
    for j in range(2 * plane):
        parcels[j] = chosen[:, j * LANES : (j + 1) * LANES]
    received[mine] = parcels[mine]

    pl.semaphore_wait(barrier, len(plane_peers) + len(z_steps))

    for step in plane_peers:
        py, px, pc = peer_of(step)
        pltpu.make_async_remote_copy(
            src_ref=parcels.at[(py * nx + px) * 2 + pc],
            dst_ref=received.at[mine],
            send_sem=parcel_sem.at[0],
            recv_sem=parcel_sem.at[1],
            device_id=(py, px, pc, z),
            device_id_type=MESH,
        ).start()
    for step in plane_peers:
        py, px, pc = peer_of(step)
        pltpu.make_async_remote_copy(
            src_ref=label_row,
            dst_ref=labels_all.at[mine],
            send_sem=label_sem.at[0],
            recv_sem=label_sem.at[1],
            device_id=(py, px, pc, z),
            device_id_type=MESH,
        ).start()
    compact = jnp.where(iota((rows, seqs * slots), 0) == row_of_slot, 1.0, 0.0)
    compact = compact.astype(jnp.bfloat16)
    others = received.at[pl.ds(0, 2 * plane - 1)]
    pltpu.make_async_copy(others, others, parcel_sem.at[1]).wait()
    block = jnp.dot(
        compact,
        received[...].reshape(seqs * slots, LANES),
        preferred_element_type=jnp.float32,
    )
    own_chip = here * nz + z
    gathered[core, own_chip] = block.astype(jnp.bfloat16)

    lane = iota((1, LANES), 1)
    lane_first = sums_before(lane, lens)
    lane_len = scatter_scalars(lane, lens)
    sub = iota((LANES, LANES), 0)
    sub_first = sums_before(sub, lens)
    sub_len = scatter_scalars(sub, lens)

    def label_table():
        row_ids = iota((LANES, LANES), 0)
        table = jnp.zeros((LANES, LANES), jnp.int32)
        for s in range(seqs):
            table = jnp.where(row_ids == s, labels_all[s], table)
        col_first = (mine * nz + z) * columns
        local = table - col_first
        code = jnp.where((local >= 0) & (local < columns), local + 1, 0)
        pieces = [code // 16, code % 16, sub_first // 16, sub_first % 16]
        return [piece.astype(jnp.float32).astype(jnp.bfloat16) for piece in pieces]

    def place_labels(pieces, zz):
        ids = nz * iota((rows, LANES), 0) + zz
        member = (ids >= lane_first) & (ids < lane_first + lane_len)
        member = jnp.where(member, 1.0, 0.0).astype(jnp.bfloat16)
        high, low, first_high, first_low = [
            jnp.dot(member, piece, preferred_element_type=jnp.float32) for piece in pieces
        ]
        position = ids.astype(jnp.float32) - (16.0 * first_high + first_low)
        at = position == iota((rows, LANES), 1).astype(jnp.float32)
        code = jnp.sum(jnp.where(at, 16.0 * high + low, 0.0), axis=1, keepdims=True)
        label_place[zz] = jnp.broadcast_to(code - 1.0, (rows, LANES))

    def multiply(chips):
        def body(turn, _):
            products = []
            for u in range(UNROLL):
                chip = chips[u]
                for t in range(1, len(chips) // UNROLL):
                    chip = jnp.where(turn == t, chips[t * UNROLL + u], chip)
                depth = pl.multiple_of((chip // nz) * (2 * LANES), 2 * LANES)
                pair = jnp.concatenate([gathered[0, chip], gathered[1, chip]], axis=1)
                products.append(
                    (
                        chip % nz,
                        jnp.dot(
                            pair,
                            weight[pl.ds(depth, 2 * LANES), :],
                            preferred_element_type=jnp.float32,
                        ),
                    )
                )
            for zz, product in products:
                scores[zz] = scores[zz] + product
            return 0

        lax.fori_loop(0, len(chips) // UNROLL, body, 0)

    plan = gather_plan(dims)
    order = {}
    for kind, node, _, _ in plan:
        if kind == "wait":
            order[node] = len(order)
    nodes = list(order)
    done = 0
    sites = 0
    pieces = None

    def wait_twin(k):
        chip = chip_of(nodes[k])
        ref = gathered.at[twin, chip]
        pltpu.make_async_copy(ref, ref, twin_recv.at[k]).wait()

    def compute(upto):
        nonlocal done, sites, pieces
        while done < upto:
            take = min(BATCH, upto - done)
            if done == 0:
                load_weight.wait()
            for k in range(done, done + take):
                wait_twin(k)
            multiply([chip_of(nodes[k]) for k in range(done, done + take)])
            if pieces is None:
                other_labels = labels_all.at[pl.ds(0, 2 * plane - 1)]
                pltpu.make_async_copy(other_labels, other_labels, label_sem.at[1]).wait()
                pieces = label_table()
            if sites < nz:
                place_labels(pieces, sites)
            done += take
            sites += 1

    for kind, node, child, way in plan:
        chip = chip_of(node)
        ref = gathered.at[core, chip]
        if kind == "wait":
            k = order[node]
            if k:
                pltpu.make_async_copy(ref, ref, block_recv.at[k]).wait()
            pltpu.make_async_remote_copy(
                src_ref=ref,
                dst_ref=ref,
                send_sem=twin_send,
                recv_sem=twin_recv.at[k],
                device_id=(y, x, twin, z),
                device_id_type=MESH,
            ).start()
            ready = k + 1 - BATCH
            if ready > done and ready - done >= BATCH:
                compute(done + BATCH)
        else:
            step = [0, 0, 0]
            step[way[0]] = way[1] % dims[way[0]]
            ty, tx, tz = shifted(*step)
            pltpu.make_async_remote_copy(
                src_ref=ref,
                dst_ref=ref,
                send_sem=block_send,
                recv_sem=block_recv.at[order[child]],
                device_id=(ty, tx, core, tz),
                device_id_type=MESH,
            ).start()
    compute(len(nodes))
    while sites < nz:
        place_labels(pieces, sites)
        sites += 1

    column_ids = iota((part_rows, columns), 1).astype(jnp.float32)
    spot = iota((part_rows, LANES), 1)
    for j in range(plane):
        zz, start = j // halves, (j % halves) * part_rows
        part = scores[zz, start : start + part_rows, :]
        code = label_place[zz, start : start + part_rows, 0:1]
        top = jnp.max(part, axis=1, keepdims=True)
        total = jnp.sum(jnp.exp(part - top), axis=1, keepdims=True)
        picked = jnp.sum(jnp.where(column_ids == code, part, 0.0), axis=1, keepdims=True)
        packed = jnp.where(
            spot == 0, top, jnp.where(spot == 1, total, jnp.where(spot == 2, picked, 0.0))
        )
        if part_rows < LANES:
            packed = jnp.concatenate(
                [packed, jnp.zeros((LANES - part_rows, LANES), jnp.float32)], axis=0
            )
        stats[j] = packed.T[0:4, :]

    plane_chips = [s for s in plane_steps if s != (0, 0)]
    stats_in[here] = stats[here]
    for a, b in plane_chips:
        py, px, _ = shifted(a, b, 0)
        pltpu.make_async_remote_copy(
            src_ref=stats.at[py * nx + px],
            dst_ref=stats_in.at[here],
            send_sem=stat_sem.at[0],
            recv_sem=stat_sem.at[1],
            device_id=(py, px, core, z),
            device_id_type=MESH,
        ).start()
    other_stats = stats_in.at[pl.ds(0, plane - 1)]
    pltpu.make_async_copy(other_stats, other_stats, stat_sem.at[1]).wait()

    def merge(ref, count):
        tops = [ref[k, 0:1, :] for k in range(count)]
        top = functools.reduce(jnp.maximum, tops)
        total = functools.reduce(
            jnp.add, [ref[k, 1:2, :] * jnp.exp(tops[k] - top) for k in range(count)]
        )
        picked = functools.reduce(jnp.add, [ref[k, 2:3, :] for k in range(count)])
        return top, total, picked

    top, total, picked = merge(stats_in, plane)
    merged[0:1, :] = top
    merged[1:2, :] = total
    merged[2:3, :] = picked
    merged[3:4, :] = jnp.zeros((1, LANES), jnp.float32)
    line = z * 2 + core
    merged_in[line] = merged[...]
    line_peers = sorted(
        [(dz, dc) for dz in range(nz) for dc in (0, 1) if (dz, dc) != (0, 0)],
        key=lambda s: -far(s[0], nz),
    )
    for dz, dc in line_peers:
        pltpu.make_async_remote_copy(
            src_ref=merged,
            dst_ref=merged_in.at[line],
            send_sem=merged_sem.at[0],
            recv_sem=merged_sem.at[1],
            device_id=(y, x, twin if dc else core, (z + dz) % nz),
            device_id_type=MESH,
        ).start()
    other_merged = merged_in.at[pl.ds(0, 2 * nz - 1)]
    pltpu.make_async_copy(other_merged, other_merged, merged_sem.at[1]).wait()

    top, total, picked = merge(merged_in, 2 * nz)
    filled = lane < part_rows
    log_norm = top + jnp.log(jnp.where(filled, total, 1.0))
    gain = jnp.where(filled, picked - log_norm, 0.0)
    row_ids = nz * ((here % halves) * part_rows + lane) + here // halves
    inside = (row_ids >= sub_first) & (row_ids < sub_first + sub_len)
    inside = jnp.where(inside, 1.0, 0.0)
    contract = (((1,), (1,)), ((), ()))
    by_seq = lax.dot_general(
        jnp.broadcast_to(gain, (8, LANES)),
        inside,
        contract,
        precision=lax.Precision.HIGHEST,
        preferred_element_type=jnp.float32,
    )[0:1, :]
    squares = jnp.sum(jnp.where(filled, log_norm * log_norm, 0.0), axis=1, keepdims=True)
    sums[...] = jnp.where(lane == seqs, squares, by_seq)
    sums_in[here] = sums[...]
    for a, b in plane_chips:
        py, px, _ = shifted(a, b, 0)
        pltpu.make_async_remote_copy(
            src_ref=sums,
            dst_ref=sums_in.at[here],
            send_sem=sums_sem.at[0],
            recv_sem=sums_sem.at[1],
            device_id=(py, px, core, z),
            device_id_type=MESH,
        ).start()
    pair_ids = iota((LANES, LANES), 0)
    select = jnp.zeros((LANES, LANES), jnp.float32)
    seq_ids = iota((LANES, LANES), 1)
    margins = jnp.zeros((1, LANES), jnp.float32)
    for p in range(pairs):
        hit = jnp.where(seq_ids == pairs_ref[2 * p], 1.0, 0.0)
        hit = hit - jnp.where(seq_ids == pairs_ref[2 * p + 1], 1.0, 0.0)
        select = jnp.where(pair_ids == p, hit, select)
        margins = jnp.where(lane == p, margins_ref[p], margins)
    live = functools.reduce(jnp.add, lens).astype(jnp.float32)

    def drain(ref, sem):
        pltpu.make_async_copy(ref, ref, sem).wait()

    drain(others, parcel_sem.at[0])
    drain(labels_all.at[pl.ds(0, 2 * plane - 1)], label_sem.at[0])
    drain(gathered.at[0, pl.ds(0, plane * nz - 1)], block_send)
    drain(gathered.at[0], twin_send)
    drain(other_stats, stat_sem.at[0])
    drain(other_merged, merged_sem.at[0])
    other_sums = sums_in.at[pl.ds(0, plane - 1)]
    drain(other_sums, sums_sem.at[1])

    row = functools.reduce(jnp.add, [sums_in[k] for k in range(plane)])
    seq_row = jnp.where(lane < seqs, row, 0.0)
    difference = lax.dot_general(
        jnp.broadcast_to(seq_row, (8, LANES)),
        select,
        contract,
        precision=lax.Precision.HIGHEST,
        preferred_element_type=jnp.float32,
    )[0:1, :]
    score = -pref_beta * (difference - margins)
    pair_row = jnp.maximum(score, 0.0) + log_one_plus(jnp.exp(-jnp.abs(score)))
    z_row = zloss_weight * row / live
    out_ref[0:1, :] = seq_row
    out_ref[1:2, :] = pair_row
    out_ref[2:3, :] = z_row
    out_ref[3:8, :] = jnp.zeros((5, LANES), jnp.float32)
    drain(other_sums, sums_sem.at[0])


def per_device(dims, hidden, head_weight, labels, lengths, pair_map, ref_margin):
    ny, nx, nz = dims
    plane = ny * nx
    window, width = hidden.shape
    columns = head_weight.shape[1]
    seqs = lengths.shape[0]
    live = seqs * window // 2
    rows = live // nz
    slots = -(-window // (nz * 16)) * 16
    bf16, f32, i32 = jnp.bfloat16, jnp.float32, jnp.int32
    vmem = pltpu.VMEM
    dma = pltpu.SemaphoreType.DMA
    out = pl.pallas_call(
        functools.partial(kernel, dims),
        out_shape=jax.ShapeDtypeStruct((8, LANES), f32),
        in_specs=[
            pl.BlockSpec(memory_space=pl.ANY),
            pl.BlockSpec(memory_space=pl.ANY),
            pl.BlockSpec(memory_space=vmem),
            pl.BlockSpec(memory_space=pltpu.SMEM),
            pl.BlockSpec(memory_space=pltpu.SMEM),
            pl.BlockSpec(memory_space=pltpu.SMEM),
        ],
        out_specs=pl.BlockSpec(memory_space=vmem),
        scratch_shapes=[
            vmem((window, width), bf16),
            vmem((width, columns), bf16),
            vmem((2 * plane, slots, LANES), bf16),
            vmem((2 * plane, slots, LANES), bf16),
            vmem((1, LANES), i32),
            vmem((2 * plane, 1, LANES), i32),
            vmem((2, plane * nz, rows, LANES), bf16),
            vmem((nz, rows, columns), f32),
            vmem((nz, rows, LANES), f32),
            vmem((plane, 4, LANES), f32),
            vmem((plane, 4, LANES), f32),
            vmem((4, LANES), f32),
            vmem((2 * nz, 4, LANES), f32),
            vmem((1, LANES), f32),
            vmem((plane, 1, LANES), f32),
            dma((2,)),
            dma((2,)),
            dma((2,)),
            dma(()),
            dma(()),
            dma((plane * nz,)),
            dma((plane * nz,)),
            dma((2,)),
            dma((2,)),
            dma((2,)),
        ],
        compiler_params=pltpu.CompilerParams(collective_id=0, has_side_effects=True),
    )(hidden, head_weight, labels.reshape(1, window), lengths, pair_map, ref_margin)
    return out[0, :seqs], out[1, : seqs // 2], out[2, seqs]


def solution(mesh):
    nz = mesh.shape["vocab"]
    ny = nx = {32: 4, 8: 2}[mesh.shape["seq"]]
    torus = Mesh(
        mesh.devices.reshape(ny, nx, 2, nz), ("seq_0", "seq_1", "seq_2", "vocab")
    )
    return jax.shard_map(
        functools.partial(per_device, (ny, nx, nz)),
        mesh=torus,
        in_specs=(P(SEQ, None), P(None, SEQ_VOCAB), P(SEQ), P(), P(), P()),
        out_specs=(P(), P(), P()),
        check_vma=False,
    )
```

time: 239 us -> 85.5 us (0.36); the launches traced: 235 us -> 85.3 us
  blocking collectives: 183 us -> 0 us
  Pallas kernels: 0 us -> 81 us
  matrix products: 19.5 us -> 0 us
  between operations: 17.5 us -> 0.64 us
  other arithmetic: 9.4 us -> 0 us
    unnamed x1 -> x0, blocking collectives: 128 us -> none
    pallas_call x0 -> x1, Pallas kernels: none -> 81 us  [per_device(): pl.pallas_call(functools.partial(kernel, dims), out_shape=jax.ShapeDtypeS...]
    all_gather x4 -> x0, blocking collectives: 55.3 us -> none  [all_in_one(): both, at, found = (lax.all_gather(jnp.concatenate(lines), axis), 0, {})]
    dot_general x2 -> x0, matrix products: 19.5 us -> none  [the longest x1 19.4 us: per_device(): jnp.dot(lax.all_gather(hidden, SEQ, axis=0, tiled=True), head_weight, pre...]
    reduce_sum x3 -> x0, other arithmetic: 6.53 us -> none  [the longest x1 3.51 us: per_device(): local_sum = jnp.sum(jnp.exp(logits - local_max[:, None]), axis=1)]
  transfers between devices with their start and end apart: 1 -> 0, of which waited for: 0 -> 0; matrix products, arithmetic and copies ran while one was open for 2% -> 0% of each run, Pallas kernels for 0% -> 0%
where the time goes in v1:
time: 85.5 us; the launch traced here: 85.3 us
  Pallas kernels  81 us (95%)
  local copies, waits for them, and re-layouts  3.65 us (4%)
    pallas_call x1, Pallas kernels, per_device(): pl.pallas_call(functools.partial(kernel, dims), out_shape=jax.ShapeDtypeS...  81 us
    squeeze x2, local copies, waits for them, and re-layouts, per_device(): return (out[0, :seqs], out[1, :seqs // 2], out[2, seqs])  2.39 us

profile of v1, /device:TPU:1, one launch (start us, length us, event | category | flops | bytes accessed | tf_op | source)
XLA Modules:
  0.0 85.3 jit_solution(11125218314420885740)
XLA Ops:
  0.6 81.0 %shard_map.85 = f32[8,128]{1,0:T(8,128)} custom-call(bf16[120,4096]{1,0:T(8,128)(2,1)} %hidden_hbm.1, bf16[4096,384]{1,0:T(8,128)(2,1)} %weight_hbm.1, s32[1,120]{1,0:T(1,128)} %bitcast.6, s32[32]{0:T(128)} %lengths_ref.1, s32[32]{0:T(128)} %pairs_ref.1, f32[16]{0:T(128)} %margins_ref.1), custom_call_target="tpu_custom_call" | custom-call | tf_op jit(solution)/shard_map/pallas_call | solution.py:554
  81.7 1.3 %slice.11 = f32[1,1]{1,0:T(1,128)} slice(f32[8,128]{1,0:T(8,128)} %shard_map.85), slice={[2:3], [32:33]} | slice | bytes 8 | tf_op jit(solution)/shard_map/slice | solution.py:595
  82.9 1.2 %slice_bitcast_fusion = f32[16]{0:T(128)} fusion(f32[8,128]{1,0:T(8,128)} %shard_map.85), kind=kLoop, calls=%fused_computation | loop fusion | bytes 128 | tf_op jit(solution)/shard_map/squeeze | solution.py:595
  84.1 1.2 %slice_bitcast_fusion.1 = f32[32]{0:T(128)} fusion(f32[8,128]{1,0:T(8,128)} %shard_map.85), kind=kLoop, calls=%fused_computation.1 | loop fusion | bytes 256 | tf_op jit(solution)/shard_map/squeeze | solution.py:595

commit v2 on v1

--- a/solution.py
+++ b/solution.py
@@ -1,5 +1,6 @@
 import functools
 import heapq
+import math
 
 import jax
 import jax.numpy as jnp
@@ -17,11 +18,23 @@
 zloss_weight = 0.0001
 
 LANES = 128
-UNROLL = 4
-BATCH = 8
-FLIGHT = 2
-WIRE = 1.32
-HOP = 1.1
+CHUNK = 4
+CUTS = 2
+BACKLOG = 1.8
+WIRE = 1.33
+HOP = 2.2
+TWIN = 1.6
+ISSUE = 0.012
+PAIR = 0.108
+PLACE = 0.35
+
+STEPS = [(0, 1), (0, -1), (1, 1), (1, -1), (2, 1), (2, -1)]
+WAYS = [
+    4, 4, 4, 5, 5, 5, 5, 2, 2, 4, 4, 4, 2, 2, 2, 3, 4, 2, 3, 5, 2, 3, 5, 3, 4, 3, 3, 3, 5, 3, 3, 0,
+    0, 4, 0, 4, 0, 5, 0, 0, 4, 0, 2, 0, 5, 0, 0, 0, 2, 2, 0, 2, 3, 3, 3, 3, 0, 3, 4, 3, 5, 0, 5, 1,
+    0, 4, 0, 0, 5, 0, 1, 1, 1, 0, 2, 1, 5, 0, 2, 3, 4, 4, 3, 2, 5, 1, 0, 1, 1, 4, 4, 5, 5, 5, 3, 1,
+    1, 4, 1, 5, 1, 1, 5, 2, 4, 1, 1, 2, 2, 1, 2, 2, 1, 2, 2, 2, 1, 5, 1, 1, 1, 3, 4, 4, 3, 5, 3,
+]
 
 
 def broadcast_tree(dims):
@@ -32,32 +45,12 @@
         for c in range(dims[2])
         if (a, b, c) != (0, 0, 0)
     ]
-    choices = {}
+    if len(nodes) == len(WAYS):
+        return {node: STEPS[way] for node, way in zip(nodes, WAYS)}
+    taken = {}
     for node in nodes:
-        ways = []
-        for axis in range(3):
-            at, size = node[axis], dims[axis]
-            if at and at <= size // 2:
-                ways.append((axis, 1))
-            if at and at >= size - size // 2:
-                ways.append((axis, -1))
-        choices[node] = ways
-    load = {}
-    taken = {}
-    for node in sorted(nodes, key=lambda n: (len(choices[n]), n)):
-        way = min(choices[node], key=lambda w: (load.get(w, 0), w))
-        taken[node] = way
-        load[way] = load.get(way, 0) + 1
-    moved = True
-    while moved:
-        moved = False
-        for node in nodes:
-            for way in choices[node]:
-                if load.get(way, 0) + 1 < load[taken[node]]:
-                    load[taken[node]] -= 1
-                    load[way] = load.get(way, 0) + 1
-                    taken[node] = way
-                    moved = True
+        axis = next(k for k in range(3) if node[k])
+        taken[node] = (axis, 1 if node[axis] <= dims[axis] // 2 else -1)
     return taken
 
 
@@ -67,7 +60,7 @@
     return tuple(place)
 
 
-def gather_plan(dims):
+def gather_plan(dims, cuts, places):
     taken = broadcast_tree(dims)
     children = {}
     for node, way in taken.items():
@@ -81,32 +74,76 @@
     def weight(node):
         return 1 + sum(weight(child) for child, _ in children.get(node, []))
 
+    wire = WIRE / cuts
     ways = sorted(set(taken.values()))
     ready = {way: [] for way in ways}
     free = {way: 0.0 for way in ways}
-    flying = {way: 0 for way in ways}
-    events = [(0.0, 0, "arrive", (0, 0, 0))]
-    count = 1
+    left = {way: cuts * sum(w == way for w in taken.values()) for way in ways}
+    arrivals = [(0.0, cut, ((0, 0, 0), cut)) for cut in range(cuts)]
+    count = cuts
+    now = 0.0
     plan = []
-    while events:
-        now, _, kind, item = heapq.heappop(events)
-        if kind == "arrive":
-            plan.append(("wait", item, None, None))
-            for child, way in children.get(item, []):
-                ready[way].append(child)
-        else:
-            flying[item] -= 1
+    arrived = {}
+    waiting = {}
+    placed = 0
+    multiplied = 0
+    cost = PAIR * CHUNK
+
+    def multiply(nodes):
+        plan.append(("multiply", tuple(nodes), None, None))
+        for node in nodes:
+            del waiting[node]
+
+    while arrivals or waiting:
+        while arrivals and arrivals[0][0] <= now:
+            piece = heapq.heappop(arrivals)[2]
+            node, cut = piece
+            plan.append(("wait", piece, None, None))
+            now += ISSUE
+            for child, way in children.get(node, []):
+                ready[way].append((child, cut))
+            arrived[node] = arrived.get(node, 0) + 1
+            if arrived[node] == cuts:
+                plan.append(("twin", node, None, None))
+                now += ISSUE
+                waiting[node] = now + TWIN
         for way in ways:
-            while ready[way] and flying[way] < FLIGHT:
-                ready[way].sort(key=lambda n: (-height(n), -weight(n), n))
-                child = ready[way].pop(0)
-                end = max(now, free[way]) + WIRE
-                free[way] = end
-                flying[way] += 1
-                plan.append(("send", before(child, way, dims), child, way))
-                heapq.heappush(events, (end, count, "sent", way))
-                heapq.heappush(events, (end + HOP, count + 1, "arrive", child))
-                count += 2
+            while ready[way] and free[way] - now < BACKLOG - 0.5 * wire:
+                ready[way].sort(key=lambda p: (-height(p[0]), -weight(p[0]), p[1], p[0]))
+                piece = ready[way].pop(0)
+                free[way] = max(now, free[way]) + wire
+                left[way] -= 1
+                plan.append(("send", (before(piece[0], way, dims), piece[1]), piece, way))
+                now += ISSUE
+                heapq.heappush(arrivals, (free[way] + HOP, count, piece))
+                count += 1
+        if arrivals and arrivals[0][0] <= now:
+            continue
+        coming = arrivals[0][0] if arrivals else math.inf
+        queued = min([free[way] - now for way in ways if left[way]], default=math.inf)
+        there = [node for node, when in waiting.items() if when <= now]
+        if len(there) >= CHUNK and (queued >= cost or coming >= now + cost or len(waiting) > 32):
+            multiply(there[:CHUNK])
+            multiplied += CHUNK
+            now += cost
+            continue
+        if placed < places and multiplied >= 2 * CHUNK:
+            if queued >= PLACE or coming >= now + PLACE:
+                plan.append(("place", placed, None, None))
+                placed += 1
+                now += PLACE
+                continue
+        later = [coming]
+        later += [free[way] - BACKLOG + 0.5 * wire for way in ways if ready[way]]
+        if len(waiting) >= CHUNK:
+            later.append(max(sorted(waiting.values())[CHUNK - 1], now + 0.05))
+        if min(later) == math.inf:
+            multiply(list(waiting)[:CHUNK])
+            now += cost
+            continue
+        now = max(now + 1e-6, min(later))
+    for k in range(placed, places):
+        plan.append(("place", k, None, None))
     return plan
 
 
@@ -145,7 +182,9 @@
     lengths_ref,
     pairs_ref,
     margins_ref,
-    out_ref,
+    seq_out,
+    pair_out,
+    z_out,
     hidden,
     weight,
     parcels,
@@ -155,6 +194,7 @@
     gathered,
     scores,
     label_place,
+    packed,
     stats,
     stats_in,
     merged,
@@ -195,11 +235,6 @@
         cy, cx, cz = shifted(-node[0] + ny, -node[1] + nx, -node[2] + nz)
         return (cy * nx + cx) * nz + cz
 
-    load_hidden = pltpu.make_async_copy(hidden_hbm, hidden, load_sem.at[0])
-    load_weight = pltpu.make_async_copy(weight_hbm, weight, load_sem.at[1])
-    load_hidden.start()
-    load_weight.start()
-
     far = lambda n, size: min(n, size - n)
     plane_steps = sorted(
         [(a, b) for a in range(ny) for b in range(nx)],
@@ -222,14 +257,11 @@
             barrier, inc=1, device_id=(y, x, core, (z + dz) % nz), device_id_type=MESH
         )
 
+    load_hidden = pltpu.make_async_copy(hidden_hbm, hidden, load_sem.at[0])
+    load_weight = pltpu.make_async_copy(weight_hbm, weight, load_sem.at[1])
+    load_hidden.start()
+
     lens = [lengths_ref[s] for s in range(seqs)]
-    slot_ids = iota((1, seqs * slots), 1)
-    slot_seq = slot_ids // slots
-    first = sums_before(slot_seq, lens)
-    place = nz * (slot_ids % slots) + ((z - first) & (nz - 1))
-    row_of_slot = jnp.where(
-        place < scatter_scalars(slot_seq, lens), (first + place - z) // nz, -1
-    )
     own_first = jnp.int32(0)
     for s in range(seqs - 1):
         own_first = own_first + jnp.where(mine > s, lens[s], 0)
@@ -239,8 +271,8 @@
     label_row[...] = jnp.zeros(label_row.shape, jnp.int32)
     label_row[0:1, 0:window] = labels_ref[...]
     labels_all[mine] = label_row[...]
-    scores[...] = jnp.zeros(scores.shape, jnp.float32)
     load_hidden.wait()
+    load_weight.start()
     chosen = jnp.dot(choose, hidden[...], preferred_element_type=jnp.float32)
     chosen = chosen.astype(jnp.bfloat16)
     for j in range(2 * plane):
@@ -269,6 +301,14 @@
             device_id=(py, px, pc, z),
             device_id_type=MESH,
         ).start()
+    slot_ids = iota((1, seqs * slots), 1)
+    slot_seq = slot_ids // slots
+    first = sums_before(slot_seq, lens)
+    place = nz * (slot_ids % slots) + ((z - first) & (nz - 1))
+    row_of_slot = jnp.where(
+        place < scatter_scalars(slot_seq, lens), (first + place - z) // nz, -1
+    )
+    scores[...] = jnp.zeros(scores.shape, jnp.float32)
     compact = jnp.where(iota((rows, seqs * slots), 0) == row_of_slot, 1.0, 0.0)
     compact = compact.astype(jnp.bfloat16)
     others = received.at[pl.ds(0, 2 * plane - 1)]
@@ -312,82 +352,50 @@
         label_place[zz] = jnp.broadcast_to(code - 1.0, (rows, LANES))
 
     def multiply(chips):
-        def body(turn, _):
-            products = []
-            for u in range(UNROLL):
-                chip = chips[u]
-                for t in range(1, len(chips) // UNROLL):
-                    chip = jnp.where(turn == t, chips[t * UNROLL + u], chip)
-                depth = pl.multiple_of((chip // nz) * (2 * LANES), 2 * LANES)
-                pair = jnp.concatenate([gathered[0, chip], gathered[1, chip]], axis=1)
-                products.append(
-                    (
-                        chip % nz,
-                        jnp.dot(
-                            pair,
-                            weight[pl.ds(depth, 2 * LANES), :],
-                            preferred_element_type=jnp.float32,
-                        ),
-                    )
-                )
-            for zz, product in products:
-                scores[zz] = scores[zz] + product
-            return 0
-
-        lax.fori_loop(0, len(chips) // UNROLL, body, 0)
-
-    plan = gather_plan(dims)
+        products = []
+        for chip in chips:
+            depth = pl.multiple_of((chip // nz) * (2 * LANES), 2 * LANES)
+            pair = jnp.concatenate([gathered[0, chip], gathered[1, chip]], axis=1)
+            product = jnp.dot(
+                pair, weight[pl.ds(depth, 2 * LANES), :], preferred_element_type=jnp.float32
+            )
+            products.append((chip % nz, product))
+        for zz, product in products:
+            scores[zz] = scores[zz] + product
+
+    edges = [0, LANES, rows] if CUTS == 2 else [0, rows]
+    plan = gather_plan(dims, CUTS, nz)
     order = {}
-    for kind, node, _, _ in plan:
+    for kind, item, _, _ in plan:
+        if kind == "twin":
+            order[item] = len(order)
+
+    def piece_ref(node, cut):
+        return gathered.at[core, chip_of(node), pl.ds(edges[cut], edges[cut + 1] - edges[cut])]
+
+    def drain(ref, sem):
+        pltpu.make_async_copy(ref, ref, sem).wait()
+
+    pieces = None
+    first_product = True
+    for kind, item, child, way in plan:
         if kind == "wait":
-            order[node] = len(order)
-    nodes = list(order)
-    done = 0
-    sites = 0
-    pieces = None
-
-    def wait_twin(k):
-        chip = chip_of(nodes[k])
-        ref = gathered.at[twin, chip]
-        pltpu.make_async_copy(ref, ref, twin_recv.at[k]).wait()
-
-    def compute(upto):
-        nonlocal done, sites, pieces
-        while done < upto:
-            take = min(BATCH, upto - done)
-            if done == 0:
-                load_weight.wait()
-            for k in range(done, done + take):
-                wait_twin(k)
-            multiply([chip_of(nodes[k]) for k in range(done, done + take)])
-            if pieces is None:
-                other_labels = labels_all.at[pl.ds(0, 2 * plane - 1)]
-                pltpu.make_async_copy(other_labels, other_labels, label_sem.at[1]).wait()
-                pieces = label_table()
-            if sites < nz:
-                place_labels(pieces, sites)
-            done += take
-            sites += 1
-
-    for kind, node, child, way in plan:
-        chip = chip_of(node)
-        ref = gathered.at[core, chip]
-        if kind == "wait":
-            k = order[node]
-            if k:
-                pltpu.make_async_copy(ref, ref, block_recv.at[k]).wait()
+            node, cut = item
+            if node != (0, 0, 0):
+                drain(piece_ref(node, cut), block_recv.at[order[node] * CUTS + cut])
+        elif kind == "twin":
+            ref = gathered.at[core, chip_of(item)]
             pltpu.make_async_remote_copy(
                 src_ref=ref,
                 dst_ref=ref,
                 send_sem=twin_send,
-                recv_sem=twin_recv.at[k],
+                recv_sem=twin_recv.at[order[item]],
                 device_id=(y, x, twin, z),
                 device_id_type=MESH,
             ).start()
-            ready = k + 1 - BATCH
-            if ready > done and ready - done >= BATCH:
-                compute(done + BATCH)
-        else:
+        elif kind == "send":
+            node, cut = item
+            ref = piece_ref(node, cut)
             step = [0, 0, 0]
             step[way[0]] = way[1] % dims[way[0]]
             ty, tx, tz = shifted(*step)
@@ -395,32 +403,39 @@
                 src_ref=ref,
                 dst_ref=ref,
                 send_sem=block_send,
-                recv_sem=block_recv.at[order[child]],
+                recv_sem=block_recv.at[order[child[0]] * CUTS + cut],
                 device_id=(ty, tx, core, tz),
                 device_id_type=MESH,
             ).start()
-    compute(len(nodes))
-    while sites < nz:
-        place_labels(pieces, sites)
-        sites += 1
-
-    column_ids = iota((part_rows, columns), 1).astype(jnp.float32)
-    spot = iota((part_rows, LANES), 1)
+        elif kind == "multiply":
+            if first_product:
+                load_weight.wait()
+                first_product = False
+            for node in item:
+                drain(gathered.at[twin, chip_of(node)], twin_recv.at[order[node]])
+            multiply([chip_of(node) for node in item])
+        else:
+            if pieces is None:
+                drain(labels_all.at[pl.ds(0, 2 * plane - 1)], label_sem.at[1])
+                pieces = label_table()
+            place_labels(pieces, item)
+
+    column_ids = iota((rows, columns), 1).astype(jnp.float32)
+    spot = iota((rows, LANES), 1)
+    for zz in range(nz):
+        top = jnp.max(scores[zz], axis=1, keepdims=True)
+        packed[zz, 0:rows, :] = jnp.broadcast_to(top, (rows, LANES))
+    for zz in range(nz):
+        part = scores[zz]
+        top = packed[zz, 0:rows, 0:1]
+        total = jnp.sum(jnp.exp(part - top), axis=1, keepdims=True)
+        hit = column_ids == label_place[zz, :, 0:1]
+        picked = jnp.sum(jnp.where(hit, part, 0.0), axis=1, keepdims=True)
+        packed[zz, 0:rows, :] = jnp.where(spot == 0, top, jnp.where(spot == 1, total, picked))
+        packed[zz, rows:, :] = jnp.zeros((LANES - part_rows, LANES), jnp.float32)
     for j in range(plane):
-        zz, start = j // halves, (j % halves) * part_rows
-        part = scores[zz, start : start + part_rows, :]
-        code = label_place[zz, start : start + part_rows, 0:1]
-        top = jnp.max(part, axis=1, keepdims=True)
-        total = jnp.sum(jnp.exp(part - top), axis=1, keepdims=True)
-        picked = jnp.sum(jnp.where(column_ids == code, part, 0.0), axis=1, keepdims=True)
-        packed = jnp.where(
-            spot == 0, top, jnp.where(spot == 1, total, jnp.where(spot == 2, picked, 0.0))
-        )
-        if part_rows < LANES:
-            packed = jnp.concatenate(
-                [packed, jnp.zeros((LANES - part_rows, LANES), jnp.float32)], axis=0
-            )
-        stats[j] = packed.T[0:4, :]
+        start = (j % halves) * part_rows
+        stats[j] = packed[j // halves, start : start + LANES, :].T[0:4, :]
 
     plane_chips = [s for s in plane_steps if s != (0, 0)]
     stats_in[here] = stats[here]
@@ -508,9 +523,6 @@
         margins = jnp.where(lane == p, margins_ref[p], margins)
     live = functools.reduce(jnp.add, lens).astype(jnp.float32)
 
-    def drain(ref, sem):
-        pltpu.make_async_copy(ref, ref, sem).wait()
-
     drain(others, parcel_sem.at[0])
     drain(labels_all.at[pl.ds(0, 2 * plane - 1)], label_sem.at[0])
     drain(gathered.at[0, pl.ds(0, plane * nz - 1)], block_send)
@@ -532,10 +544,9 @@
     score = -pref_beta * (difference - margins)
     pair_row = jnp.maximum(score, 0.0) + log_one_plus(jnp.exp(-jnp.abs(score)))
     z_row = zloss_weight * row / live
-    out_ref[0:1, :] = seq_row
-    out_ref[1:2, :] = pair_row
-    out_ref[2:3, :] = z_row
-    out_ref[3:8, :] = jnp.zeros((5, LANES), jnp.float32)
+    seq_out[...] = seq_row[:, :seqs]
+    pair_out[...] = pair_row[:, :pairs]
+    z_out[...] = z_row[:, seqs : seqs + 1]
     drain(other_sums, sums_sem.at[0])
 
 
@@ -551,9 +562,9 @@
     bf16, f32, i32 = jnp.bfloat16, jnp.float32, jnp.int32
     vmem = pltpu.VMEM
     dma = pltpu.SemaphoreType.DMA
-    out = pl.pallas_call(
+    seq_logps, pair_loss, z_loss = pl.pallas_call(
         functools.partial(kernel, dims),
-        out_shape=jax.ShapeDtypeStruct((8, LANES), f32),
+        out_shape=[jax.ShapeDtypeStruct((1, n), f32) for n in (seqs, seqs // 2, 1)],
         in_specs=[
             pl.BlockSpec(memory_space=pl.ANY),
             pl.BlockSpec(memory_space=pl.ANY),
@@ -562,7 +573,7 @@
             pl.BlockSpec(memory_space=pltpu.SMEM),
             pl.BlockSpec(memory_space=pltpu.SMEM),
         ],
-        out_specs=pl.BlockSpec(memory_space=vmem),
+        out_specs=[pl.BlockSpec(memory_space=vmem)] * 3,
         scratch_shapes=[
             vmem((window, width), bf16),
             vmem((width, columns), bf16),
@@ -573,6 +584,7 @@
             vmem((2, plane * nz, rows, LANES), bf16),
             vmem((nz, rows, columns), f32),
             vmem((nz, rows, LANES), f32),
+            vmem((nz, rows - rows * nz // plane + LANES, LANES), f32),
             vmem((plane, 4, LANES), f32),
             vmem((plane, 4, LANES), f32),
             vmem((4, LANES), f32),
@@ -584,7 +596,7 @@
             dma((2,)),
             dma(()),
             dma(()),
-            dma((plane * nz,)),
+            dma((CUTS * plane * nz,)),
             dma((plane * nz,)),
             dma((2,)),
             dma((2,)),
@@ -592,7 +604,7 @@
         ],
         compiler_params=pltpu.CompilerParams(collective_id=0, has_side_effects=True),
     )(hidden, head_weight, labels.reshape(1, window), lengths, pair_map, ref_margin)
-    return out[0, :seqs], out[1, : seqs // 2], out[2, seqs]
+    return seq_logps.reshape(seqs), pair_loss.reshape(seqs // 2), z_loss.reshape(())
 
 
 def solution(mesh):

time: 85.5 us -> 78.4 us (0.917)
  Pallas kernels: 81 us -> 73.6 us
  between operations: 0.64 us -> 2.4 us
  local copies, waits for them, and re-layouts: 3.65 us -> 2.25 us
    pallas_call x1, Pallas kernels: 81 us -> 73.6 us  [per_device(): pl.pallas_call(functools.partial(kernel, dims), out_shape=[jax.ShapeDtype...]
    squeeze x2 -> x0, local copies, waits for them, and re-layouts: 2.39 us -> none  [per_device(): return (out[0, :seqs], out[1, :seqs // 2], out[2, seqs])]
    unnamed x0 -> x2, local copies, waits for them, and re-layouts: none -> 2.25 us
    slice x1 -> x0, local copies, waits for them, and re-layouts: 1.26 us -> none  [per_device(): return (out[0, :seqs], out[1, :seqs // 2], out[2, seqs])]
where the time goes in v2:
time: 78.4 us; the launch traced here: 78.2 us
  Pallas kernels  73.6 us (94%)
  between operations  2.4 us (3%)
  local copies, waits for them, and re-layouts  2.25 us (3%)
    pallas_call x1, Pallas kernels, per_device(): pl.pallas_call(functools.partial(kernel, dims), out_shape=[jax.ShapeDtype...  73.6 us
    unnamed x2, local copies, waits for them, and re-layouts  2.25 us

profile of v2, /device:TPU:1, one launch (start us, length us, event | category | flops | bytes accessed | tf_op | source)
XLA Modules:
  0.0 78.2 jit_solution(2956644456033525826)
XLA Ops:
  0.6 73.6 %shard_map.85 = (f32[1,32]{1,0:T(1,128)}, f32[1,16]{1,0:T(1,128)}, f32[1,1]{1,0:T(1,128)}) custom-call(bf16[120,4096]{1,0:T(8,128)(2,1)} %hidden_hbm.1, bf16[4096,384]{1,0:T(8,128)(2,1)} %weight_hbm.1, s32[1,120]{1,0:T(1,128)} %bitcast.4, s32[32]{0:T(128)} %lengths_ref.1, s32[32]{0:T(128)} %pairs_ref.1, f32[16]{0:T(128)} %margins_ref.1), custom_call_target="tpu_custom_call" | custom-call | tf_op jit(solution)/shard_map/pallas_call | solution.py:565
  74.2 1.1 %copy.12 = f32[32]{0:T(128)} copy(f32[32]{0:T(128)} %bitcast.6) | data formatting | bytes 256
  75.3 1.1 %copy.13 = f32[16]{0:T(128)} copy(f32[16]{0:T(128)} %bitcast.5) | data formatting | bytes 128

commit v3 on v2

--- a/solution.py
+++ b/solution.py
@@ -27,6 +27,7 @@
 ISSUE = 0.012
 PAIR = 0.108
 PLACE = 0.35
+STATS = 0.35
 
 STEPS = [(0, 1), (0, -1), (1, 1), (1, -1), (2, 1), (2, -1)]
 WAYS = [
@@ -60,7 +61,7 @@
     return tuple(place)
 
 
-def gather_plan(dims, cuts, places):
+def gather_plan(dims, cuts):
     taken = broadcast_tree(dims)
     children = {}
     for node, way in taken.items():
@@ -85,14 +86,24 @@
     plan = []
     arrived = {}
     waiting = {}
-    placed = 0
     multiplied = 0
     cost = PAIR * CHUNK
+    ranks = sorted(range(dims[2]), key=lambda dz: (min(dz, dims[2] - dz), dz))
+    places = list(ranks)
+    missing = {dz: dims[0] * dims[1] for dz in ranks}
+    finished = []
 
     def multiply(nodes):
         plan.append(("multiply", tuple(nodes), None, None))
         for node in nodes:
             del waiting[node]
+            missing[node[2]] -= 1
+            if not missing[node[2]]:
+                finished.append(node[2])
+
+    def urgency(piece):
+        node, cut = piece
+        return (-height(node), -weight(node), ranks.index(node[2]), cut, node)
 
     while arrivals or waiting:
         while arrivals and arrivals[0][0] <= now:
@@ -109,7 +120,7 @@
                 waiting[node] = now + TWIN
         for way in ways:
             while ready[way] and free[way] - now < BACKLOG - 0.5 * wire:
-                ready[way].sort(key=lambda p: (-height(p[0]), -weight(p[0]), p[1], p[0]))
+                ready[way].sort(key=urgency)
                 piece = ready[way].pop(0)
                 free[way] = max(now, free[way]) + wire
                 left[way] -= 1
@@ -122,15 +133,20 @@
         coming = arrivals[0][0] if arrivals else math.inf
         queued = min([free[way] - now for way in ways if left[way]], default=math.inf)
         there = [node for node, when in waiting.items() if when <= now]
+        there.sort(key=lambda node: ranks.index(node[2]))
+        if finished and finished[0] not in places:
+            if queued >= STATS or coming >= now + STATS:
+                plan.append(("stats", finished.pop(0), None, None))
+                now += STATS
+                continue
         if len(there) >= CHUNK and (queued >= cost or coming >= now + cost or len(waiting) > 32):
             multiply(there[:CHUNK])
             multiplied += CHUNK
             now += cost
             continue
-        if placed < places and multiplied >= 2 * CHUNK:
+        if places and multiplied >= 2 * CHUNK:
             if queued >= PLACE or coming >= now + PLACE:
-                plan.append(("place", placed, None, None))
-                placed += 1
+                plan.append(("place", places.pop(0), None, None))
                 now += PLACE
                 continue
         later = [coming]
@@ -142,8 +158,10 @@
             now += cost
             continue
         now = max(now + 1e-6, min(later))
-    for k in range(placed, places):
-        plan.append(("place", k, None, None))
+    for dz in places:
+        plan.append(("place", dz, None, None))
+    for dz in finished:
+        plan.append(("stats", dz, None, None))
     return plan
 
 
@@ -235,6 +253,10 @@
         cy, cx, cz = shifted(-node[0] + ny, -node[1] + nx, -node[2] + nz)
         return (cy * nx + cx) * nz + cz
 
+    load_hidden = pltpu.make_async_copy(hidden_hbm, hidden, load_sem.at[0])
+    load_weight = pltpu.make_async_copy(weight_hbm, weight, load_sem.at[1])
+    load_hidden.start()
+
     far = lambda n, size: min(n, size - n)
     plane_steps = sorted(
         [(a, b) for a in range(ny) for b in range(nx)],
@@ -256,10 +278,6 @@
         pl.semaphore_signal(
             barrier, inc=1, device_id=(y, x, core, (z + dz) % nz), device_id_type=MESH
         )
-
-    load_hidden = pltpu.make_async_copy(hidden_hbm, hidden, load_sem.at[0])
-    load_weight = pltpu.make_async_copy(weight_hbm, weight, load_sem.at[1])
-    load_hidden.start()
 
     lens = [lengths_ref[s] for s in range(seqs)]
     own_first = jnp.int32(0)
@@ -363,8 +381,42 @@
         for zz, product in products:
             scores[zz] = scores[zz] + product
 
+    spot = iota((rows, LANES), 1)
+
+    def summarize(zz):
+        tiles = [scores[zz, :, k : k + LANES] for k in range(0, columns, LANES)]
+        top = jnp.max(functools.reduce(jnp.maximum, tiles), axis=1, keepdims=True)
+        total = functools.reduce(jnp.add, [jnp.exp(tile - top) for tile in tiles])
+        total = jnp.sum(total, axis=1, keepdims=True)
+        code = label_place[zz]
+        picked = functools.reduce(
+            jnp.add,
+            [
+                jnp.where(code - float(k * LANES) == spot.astype(jnp.float32), tile, 0.0)
+                for k, tile in enumerate(tiles)
+            ],
+        )
+        picked = jnp.sum(picked, axis=1, keepdims=True)
+        packed[0:rows, :] = jnp.where(spot == 0, top, jnp.where(spot == 1, total, picked))
+        for half in range(halves):
+            j = zz * halves + half
+            start = half * part_rows
+            stats[j] = packed[start : start + LANES, :].T[0:4, :]
+
+            @pl.when(j != here)
+            def _():
+                pltpu.make_async_remote_copy(
+                    src_ref=stats.at[j],
+                    dst_ref=stats_in.at[here],
+                    send_sem=stat_sem.at[0],
+                    recv_sem=stat_sem.at[1],
+                    device_id=(j // nx, j % nx, core, z),
+                    device_id_type=MESH,
+                ).start()
+
+    packed[rows:, :] = jnp.zeros((LANES - part_rows, LANES), jnp.float32)
     edges = [0, LANES, rows] if CUTS == 2 else [0, rows]
-    plan = gather_plan(dims, CUTS, nz)
+    plan = gather_plan(dims, CUTS)
     order = {}
     for kind, item, _, _ in plan:
         if kind == "twin":
@@ -414,41 +466,16 @@
             for node in item:
                 drain(gathered.at[twin, chip_of(node)], twin_recv.at[order[node]])
             multiply([chip_of(node) for node in item])
+        elif kind == "stats":
+            summarize((z + nz - item) % nz)
         else:
             if pieces is None:
                 drain(labels_all.at[pl.ds(0, 2 * plane - 1)], label_sem.at[1])
                 pieces = label_table()
-            place_labels(pieces, item)
-
-    column_ids = iota((rows, columns), 1).astype(jnp.float32)
-    spot = iota((rows, LANES), 1)
-    for zz in range(nz):
-        top = jnp.max(scores[zz], axis=1, keepdims=True)
-        packed[zz, 0:rows, :] = jnp.broadcast_to(top, (rows, LANES))
-    for zz in range(nz):
-        part = scores[zz]
-        top = packed[zz, 0:rows, 0:1]
-        total = jnp.sum(jnp.exp(part - top), axis=1, keepdims=True)
-        hit = column_ids == label_place[zz, :, 0:1]
-        picked = jnp.sum(jnp.where(hit, part, 0.0), axis=1, keepdims=True)
-        packed[zz, 0:rows, :] = jnp.where(spot == 0, top, jnp.where(spot == 1, total, picked))
-        packed[zz, rows:, :] = jnp.zeros((LANES - part_rows, LANES), jnp.float32)
-    for j in range(plane):
-        start = (j % halves) * part_rows
-        stats[j] = packed[j // halves, start : start + LANES, :].T[0:4, :]
+            place_labels(pieces, (z + nz - item) % nz)
 
     plane_chips = [s for s in plane_steps if s != (0, 0)]
     stats_in[here] = stats[here]
-    for a, b in plane_chips:
-        py, px, _ = shifted(a, b, 0)
-        pltpu.make_async_remote_copy(
-            src_ref=stats.at[py * nx + px],
-            dst_ref=stats_in.at[here],
-            send_sem=stat_sem.at[0],
-            recv_sem=stat_sem.at[1],
-            device_id=(py, px, core, z),
-            device_id_type=MESH,
-        ).start()
     other_stats = stats_in.at[pl.ds(0, plane - 1)]
     pltpu.make_async_copy(other_stats, other_stats, stat_sem.at[1]).wait()
 
@@ -584,7 +611,7 @@
             vmem((2, plane * nz, rows, LANES), bf16),
             vmem((nz, rows, columns), f32),
             vmem((nz, rows, LANES), f32),
-            vmem((nz, rows - rows * nz // plane + LANES, LANES), f32),
+            vmem((rows - rows * nz // plane + LANES, LANES), f32),
             vmem((plane, 4, LANES), f32),
             vmem((plane, 4, LANES), f32),
             vmem((4, LANES), f32),

time: 78.4 us -> 74.5 us (0.950)
  Pallas kernels: 73.6 us -> 69.7 us
    pallas_call x1, Pallas kernels: 73.6 us -> 69.7 us  [per_device(): pl.pallas_call(functools.partial(kernel, dims), out_shape=[jax.ShapeDtype...]
where the time goes in v3:
time: 74.5 us; the launch traced here: 74.3 us
  Pallas kernels  69.7 us (94%)
  between operations  2.4 us (3%)
  local copies, waits for them, and re-layouts  2.25 us (3%)
    pallas_call x1, Pallas kernels, per_device(): pl.pallas_call(functools.partial(kernel, dims), out_shape=[jax.ShapeDtype...  69.7 us
    unnamed x2, local copies, waits for them, and re-layouts  2.25 us

profile of v3, /device:TPU:1, one launch (start us, length us, event | category | flops | bytes accessed | tf_op | source)
XLA Modules:
  0.0 74.3 jit_solution(5400370936014582557)
XLA Ops:
  0.6 69.7 %shard_map.85 = (f32[1,32]{1,0:T(1,128)}, f32[1,16]{1,0:T(1,128)}, f32[1,1]{1,0:T(1,128)}) custom-call(bf16[120,4096]{1,0:T(8,128)(2,1)} %hidden_hbm.1, bf16[4096,384]{1,0:T(8,128)(2,1)} %weight_hbm.1, s32[1,120]{1,0:T(1,128)} %bitcast.4, s32[32]{0:T(128)} %lengths_ref.1, s32[32]{0:T(128)} %pairs_ref.1, f32[16]{0:T(128)} %margins_ref.1), custom_call_target="tpu_custom_call" | custom-call | tf_op jit(solution)/shard_map/pallas_call | solution.py:592
  70.3 1.1 %copy.12 = f32[32]{0:T(128)} copy(f32[32]{0:T(128)} %bitcast.6) | data formatting | bytes 256
  71.4 1.1 %copy.13 = f32[16]{0:T(128)} copy(f32[16]{0:T(128)} %bitcast.5) | data formatting | bytes 128

commit v4 on v3

--- a/solution.py
+++ b/solution.py
@@ -200,9 +200,7 @@
     lengths_ref,
     pairs_ref,
     margins_ref,
-    seq_out,
-    pair_out,
-    z_out,
+    out_ref,
     hidden,
     weight,
     parcels,
@@ -238,13 +236,16 @@
     slots = parcels.shape[1]
     rows = gathered.shape[2]
     columns = weight.shape[1]
-    halves = plane // nz
-    part_rows = rows // halves
+    part_rows = 15 * LANES // 16
+    parts = rows // part_rows
+    pack = nz // nx
+    owners = 2 * nx
     y, x = lax.axis_index("seq_0"), lax.axis_index("seq_1")
     core, z = lax.axis_index("seq_2"), lax.axis_index("vocab")
     here = y * nx + x
     mine = here * 2 + core
     twin = 1 - core
+    rank = x * 2 + core
 
     def shifted(dy, dx, dz):
         return ((y + dy) % ny, (x + dx) % nx, (z + dz) % nz)
@@ -397,22 +398,25 @@
             ],
         )
         picked = jnp.sum(picked, axis=1, keepdims=True)
-        packed[0:rows, :] = jnp.where(spot == 0, top, jnp.where(spot == 1, total, picked))
-        for half in range(halves):
-            j = zz * halves + half
-            start = half * part_rows
-            stats[j] = packed[start : start + LANES, :].T[0:4, :]
-
-            @pl.when(j != here)
-            def _():
-                pltpu.make_async_remote_copy(
-                    src_ref=stats.at[j],
-                    dst_ref=stats_in.at[here],
-                    send_sem=stat_sem.at[0],
-                    recv_sem=stat_sem.at[1],
-                    device_id=(j // nx, j % nx, core, z),
-                    device_id_type=MESH,
-                ).start()
+        packed[0:rows, :] = jnp.where(spot == 0, top + jnp.log(total), picked)
+        for part in range(parts):
+            flat = packed[part * part_rows : part * part_rows + LANES, :].T
+            slot = part % pack
+            owner = zz * (parts // pack) + part // pack
+            stats[owner, slot : slot + 1, :] = flat[0:1, :]
+            stats[owner, pack + slot : pack + slot + 1, :] = flat[1:2, :]
+            if slot == pack - 1:
+
+                @pl.when(owner != rank)
+                def _():
+                    pltpu.make_async_remote_copy(
+                        src_ref=stats.at[owner],
+                        dst_ref=stats_in.at[rank],
+                        send_sem=stat_sem.at[0],
+                        recv_sem=stat_sem.at[1],
+                        device_id=(y, owner // 2, owner % 2, z),
+                        device_id_type=MESH,
+                    ).start()
 
     packed[rows:, :] = jnp.zeros((LANES - part_rows, LANES), jnp.float32)
     edges = [0, LANES, rows] if CUTS == 2 else [0, rows]
@@ -474,71 +478,78 @@
                 pieces = label_table()
             place_labels(pieces, (z + nz - item) % nz)
 
-    plane_chips = [s for s in plane_steps if s != (0, 0)]
-    stats_in[here] = stats[here]
-    other_stats = stats_in.at[pl.ds(0, plane - 1)]
-    pltpu.make_async_copy(other_stats, other_stats, stat_sem.at[1]).wait()
-
-    def merge(ref, count):
-        tops = [ref[k, 0:1, :] for k in range(count)]
-        top = functools.reduce(jnp.maximum, tops)
-        total = functools.reduce(
-            jnp.add, [ref[k, 1:2, :] * jnp.exp(tops[k] - top) for k in range(count)]
+    def merge(ref, slot):
+        several = ref[:, slot, :]
+        top = jnp.max(several, axis=0, keepdims=True)
+        return top + jnp.log(jnp.sum(jnp.exp(several - top), axis=0, keepdims=True))
+
+    filled = lane < part_rows
+    insides = []
+    for slot in range(pack):
+        part = rank * pack + slot
+        row_ids = nz * ((part % parts) * part_rows + lane) + part // parts
+        inside = (row_ids >= sub_first) & (row_ids < sub_first + sub_len)
+        insides.append(jnp.where(inside, 1.0, 0.0))
+    contract = (((1,), (1,)), ((), ()))
+
+    stats_in[rank] = stats[rank]
+    other_stats = stats_in.at[pl.ds(0, owners - 1)]
+    drain(other_stats, stat_sem.at[1])
+    merged[...] = jnp.zeros(merged.shape, jnp.float32)
+    for slot in range(pack):
+        merged[slot : slot + 1, :] = merge(stats_in, slot)
+        merged[pack + slot : pack + slot + 1, :] = jnp.sum(
+            stats_in[:, pack + slot, :], axis=0, keepdims=True
         )
-        picked = functools.reduce(jnp.add, [ref[k, 2:3, :] for k in range(count)])
-        return top, total, picked
-
-    top, total, picked = merge(stats_in, plane)
-    merged[0:1, :] = top
-    merged[1:2, :] = total
-    merged[2:3, :] = picked
-    merged[3:4, :] = jnp.zeros((1, LANES), jnp.float32)
-    line = z * 2 + core
-    merged_in[line] = merged[...]
-    line_peers = sorted(
-        [(dz, dc) for dz in range(nz) for dc in (0, 1) if (dz, dc) != (0, 0)],
-        key=lambda s: -far(s[0], nz),
+    sheet = y * nz + z
+    merged_in[sheet] = merged[...]
+    sheet_peers = sorted(
+        [(dy, dz) for dy in range(ny) for dz in range(nz) if (dy, dz) != (0, 0)],
+        key=lambda s: -far(s[0], ny) - far(s[1], nz),
     )
-    for dz, dc in line_peers:
+    for dy, dz in sheet_peers:
+        ty, _, tz = shifted(dy, 0, dz)
         pltpu.make_async_remote_copy(
             src_ref=merged,
-            dst_ref=merged_in.at[line],
+            dst_ref=merged_in.at[sheet],
             send_sem=merged_sem.at[0],
             recv_sem=merged_sem.at[1],
-            device_id=(y, x, twin if dc else core, (z + dz) % nz),
+            device_id=(ty, x, core, tz),
             device_id_type=MESH,
         ).start()
-    other_merged = merged_in.at[pl.ds(0, 2 * nz - 1)]
-    pltpu.make_async_copy(other_merged, other_merged, merged_sem.at[1]).wait()
-
-    top, total, picked = merge(merged_in, 2 * nz)
-    filled = lane < part_rows
-    log_norm = top + jnp.log(jnp.where(filled, total, 1.0))
-    gain = jnp.where(filled, picked - log_norm, 0.0)
-    row_ids = nz * ((here % halves) * part_rows + lane) + here // halves
-    inside = (row_ids >= sub_first) & (row_ids < sub_first + sub_len)
-    inside = jnp.where(inside, 1.0, 0.0)
-    contract = (((1,), (1,)), ((), ()))
-    by_seq = lax.dot_general(
-        jnp.broadcast_to(gain, (8, LANES)),
-        inside,
-        contract,
-        precision=lax.Precision.HIGHEST,
-        preferred_element_type=jnp.float32,
-    )[0:1, :]
-    squares = jnp.sum(jnp.where(filled, log_norm * log_norm, 0.0), axis=1, keepdims=True)
+    other_merged = merged_in.at[pl.ds(0, ny * nz - 1)]
+    drain(other_merged, merged_sem.at[1])
+
+    by_seq = jnp.zeros((1, LANES), jnp.float32)
+    squares = jnp.zeros((1, LANES), jnp.float32)
+    for slot in range(pack):
+        log_norm = merge(merged_in, slot)
+        picked = jnp.sum(merged_in[:, pack + slot, :], axis=0, keepdims=True)
+        gain = jnp.where(filled, picked - log_norm, 0.0)
+        by_seq = by_seq + lax.dot_general(
+            jnp.broadcast_to(gain, (8, LANES)),
+            insides[slot],
+            contract,
+            precision=lax.Precision.HIGHEST,
+            preferred_element_type=jnp.float32,
+        )[0:1, :]
+        squares = squares + jnp.where(filled, log_norm * log_norm, 0.0)
+    squares = jnp.sum(squares, axis=1, keepdims=True)
     sums[...] = jnp.where(lane == seqs, squares, by_seq)
-    sums_in[here] = sums[...]
-    for a, b in plane_chips:
-        py, px, _ = shifted(a, b, 0)
-        pltpu.make_async_remote_copy(
-            src_ref=sums,
-            dst_ref=sums_in.at[here],
-            send_sem=sums_sem.at[0],
-            recv_sem=sums_sem.at[1],
-            device_id=(py, px, core, z),
-            device_id_type=MESH,
-        ).start()
+    sums_in[rank] = sums[...]
+    for dx in sorted(range(nx), key=lambda d: -far(d, nx)):
+        for dc in (0, 1):
+            if (dx, dc) == (0, 0):
+                continue
+            _, tx, _ = shifted(0, dx, 0)
+            pltpu.make_async_remote_copy(
+                src_ref=sums,
+                dst_ref=sums_in.at[rank],
+                send_sem=sums_sem.at[0],
+                recv_sem=sums_sem.at[1],
+                device_id=(y, tx, twin if dc else core, z),
+                device_id_type=MESH,
+            ).start()
     pair_ids = iota((LANES, LANES), 0)
     select = jnp.zeros((LANES, LANES), jnp.float32)
     seq_ids = iota((LANES, LANES), 1)
@@ -556,10 +567,10 @@
     drain(gathered.at[0], twin_send)
     drain(other_stats, stat_sem.at[0])
     drain(other_merged, merged_sem.at[0])
-    other_sums = sums_in.at[pl.ds(0, plane - 1)]
+    other_sums = sums_in.at[pl.ds(0, owners - 1)]
     drain(other_sums, sums_sem.at[1])
 
-    row = functools.reduce(jnp.add, [sums_in[k] for k in range(plane)])
+    row = functools.reduce(jnp.add, [sums_in[k] for k in range(owners)])
     seq_row = jnp.where(lane < seqs, row, 0.0)
     difference = lax.dot_general(
         jnp.broadcast_to(seq_row, (8, LANES)),
@@ -571,10 +582,18 @@
     score = -pref_beta * (difference - margins)
     pair_row = jnp.maximum(score, 0.0) + log_one_plus(jnp.exp(-jnp.abs(score)))
     z_row = zloss_weight * row / live
-    seq_out[...] = seq_row[:, :seqs]
-    pair_out[...] = pair_row[:, :pairs]
-    z_out[...] = z_row[:, seqs : seqs + 1]
+    out_ref[0:1, :] = seq_row
+    out_ref[1:2, :] = pair_row
+    out_ref[2:3, :] = z_row
+    out_ref[3:8, :] = jnp.zeros((5, LANES), jnp.float32)
     drain(other_sums, sums_sem.at[0])
+
+
+def split_results(results_ref, seq_out, pair_out, z_out):
+    seqs = seq_out.shape[1]
+    seq_out[...] = results_ref[0:1, :seqs]
+    pair_out[...] = results_ref[1:2, : pair_out.shape[1]]
+    z_out[...] = results_ref[2:3, seqs : seqs + 1]
 
 
 def per_device(dims, hidden, head_weight, labels, lengths, pair_map, ref_margin):
@@ -589,9 +608,9 @@
     bf16, f32, i32 = jnp.bfloat16, jnp.float32, jnp.int32
     vmem = pltpu.VMEM
     dma = pltpu.SemaphoreType.DMA
-    seq_logps, pair_loss, z_loss = pl.pallas_call(
+    results = pl.pallas_call(
         functools.partial(kernel, dims),
-        out_shape=[jax.ShapeDtypeStruct((1, n), f32) for n in (seqs, seqs // 2, 1)],
+        out_shape=jax.ShapeDtypeStruct((8, LANES), f32),
         in_specs=[
             pl.BlockSpec(memory_space=pl.ANY),
             pl.BlockSpec(memory_space=pl.ANY),
@@ -600,7 +619,7 @@
             pl.BlockSpec(memory_space=pltpu.SMEM),
             pl.BlockSpec(memory_space=pltpu.SMEM),
         ],
-        out_specs=[pl.BlockSpec(memory_space=vmem)] * 3,
+        out_specs=pl.BlockSpec(memory_space=vmem),
         scratch_shapes=[
             vmem((window, width), bf16),
             vmem((width, columns), bf16),
@@ -611,13 +630,13 @@
             vmem((2, plane * nz, rows, LANES), bf16),
             vmem((nz, rows, columns), f32),
             vmem((nz, rows, LANES), f32),
-            vmem((rows - rows * nz // plane + LANES, LANES), f32),
-            vmem((plane, 4, LANES), f32),
-            vmem((plane, 4, LANES), f32),
+            vmem((rows + LANES // 16, LANES), f32),
+            vmem((2 * nx, 4, LANES), f32),
+            vmem((2 * nx, 4, LANES), f32),
             vmem((4, LANES), f32),
-            vmem((2 * nz, 4, LANES), f32),
+            vmem((ny * nz, 4, LANES), f32),
             vmem((1, LANES), f32),
-            vmem((plane, 1, LANES), f32),
+            vmem((2 * nx, 1, LANES), f32),
             dma((2,)),
             dma((2,)),
             dma((2,)),
@@ -631,6 +650,12 @@
         ],
         compiler_params=pltpu.CompilerParams(collective_id=0, has_side_effects=True),
     )(hidden, head_weight, labels.reshape(1, window), lengths, pair_map, ref_margin)
+    seq_logps, pair_loss, z_loss = pl.pallas_call(
+        split_results,
+        out_shape=[jax.ShapeDtypeStruct((1, n), f32) for n in (seqs, seqs // 2, 1)],
+        in_specs=[pl.BlockSpec(memory_space=vmem)],
+        out_specs=[pl.BlockSpec(memory_space=vmem)] * 3,
+    )(results)
     return seq_logps.reshape(seqs), pair_loss.reshape(seqs // 2), z_loss.reshape(())
 
 

time: 74.5 us -> 70.4 us (0.945)
  local copies, waits for them, and re-layouts: 2.25 us -> 0 us
  between operations: 2.4 us -> 0.64 us
    unnamed x2 -> x0, local copies, waits for them, and re-layouts: 2.25 us -> none
    pallas_call x1 -> x2, Pallas kernels: 69.7 us -> 69.6 us  [the longest x1 68.3 us: per_device(): pl.pallas_call(functools.partial(kernel, dims), out_shape=jax.ShapeDtypeS...]
where the time goes in v4:
time: 70.4 us; the launch traced here: 70.2 us
  Pallas kernels  69.6 us (99%)
    pallas_call x1, Pallas kernels, per_device(): pl.pallas_call(functools.partial(kernel, dims), out_shape=jax.ShapeDtypeS...  68.3 us

profile of v4, /device:TPU:1, one launch (start us, length us, event | category | flops | bytes accessed | tf_op | source)
XLA Modules:
  0.0 70.2 jit_solution(3979875699555931687)
XLA Ops:
  0.6 68.3 %shard_map.85.results_ref = f32[8,128]{1,0:T(8,128)} custom-call(bf16[120,4096]{1,0:T(8,128)(2,1)} %hidden_hbm.1, bf16[4096,384]{1,0:T(8,128)(2,1)} %weight_hbm.1, s32[1,120]{1,0:T(1,128)} %bitcast.4, s32[32]{0:T(128)} %lengths_ref.1, s32[32]{0:T(128)} %pairs_ref.1, f32[16]{0:T(128)} %margins_ref.1), custom_call_target="tpu_custom_call" | custom-call | tf_op jit(solution)/shard_map/pallas_call | solution.py:611
  69.0 1.3 %shard_map.86 = (f32[1,32]{1,0:T(1,128)}, f32[1,16]{1,0:T(1,128)}, f32[1,1]{1,0:T(1,128)}) custom-call(f32[8,128]{1,0:T(8,128)} %shard_map.85.results_ref), custom_call_target="tpu_custom_call" | custom-call | tf_op jit(solution)/shard_map/pallas_call | solution.py:653

commit v5 on v4

--- a/solution.py
+++ b/solution.py
@@ -196,11 +196,15 @@
     dims,
     hidden_hbm,
     weight_hbm,
+    labels_hbm,
+    lengths_hbm,
+    pairs_hbm,
+    margins_hbm,
+    out_ref,
     labels_ref,
     lengths_ref,
     pairs_ref,
     margins_ref,
-    out_ref,
     hidden,
     weight,
     parcels,
@@ -257,6 +261,14 @@
     load_hidden = pltpu.make_async_copy(hidden_hbm, hidden, load_sem.at[0])
     load_weight = pltpu.make_async_copy(weight_hbm, weight, load_sem.at[1])
     load_hidden.start()
+    small = [(lengths_hbm, lengths_ref), (labels_hbm, labels_ref)]
+    small += [(pairs_hbm, pairs_ref), (margins_hbm, margins_ref)]
+    load_small = [
+        pltpu.make_async_copy(source, target, load_sem.at[2 + k])
+        for k, (source, target) in enumerate(small)
+    ]
+    for copy in load_small:
+        copy.start()
 
     far = lambda n, size: min(n, size - n)
     plane_steps = sorted(
@@ -280,6 +292,8 @@
             barrier, inc=1, device_id=(y, x, core, (z + dz) % nz), device_id_type=MESH
         )
 
+    for copy in load_small:
+        copy.wait()
     lens = [lengths_ref[s] for s in range(seqs)]
     own_first = jnp.int32(0)
     for s in range(seqs - 1):
@@ -483,13 +497,24 @@
         top = jnp.max(several, axis=0, keepdims=True)
         return top + jnp.log(jnp.sum(jnp.exp(several - top), axis=0, keepdims=True))
 
+    pair_ids = iota((LANES, LANES), 0)
+    select = jnp.zeros((LANES, LANES), jnp.float32)
+    seq_ids = iota((LANES, LANES), 1)
+    margins = jnp.zeros((1, LANES), jnp.float32)
+    for p in range(pairs):
+        hit = jnp.where(seq_ids == pairs_ref[2 * p], 1.0, 0.0)
+        hit = hit - jnp.where(seq_ids == pairs_ref[2 * p + 1], 1.0, 0.0)
+        select = jnp.where(pair_ids == p, hit, select)
+        margins = jnp.where(lane == p, margins_ref[p], margins)
     filled = lane < part_rows
     insides = []
     for slot in range(pack):
         part = rank * pack + slot
         row_ids = nz * ((part % parts) * part_rows + lane) + part // parts
         inside = (row_ids >= sub_first) & (row_ids < sub_first + sub_len)
-        insides.append(jnp.where(inside, 1.0, 0.0))
+        inside = jnp.where(inside, 1.0, 0.0)
+        by_pair = jnp.dot(select, inside, preferred_element_type=jnp.float32)
+        insides.append(jnp.concatenate([inside, by_pair], axis=0))
     contract = (((1,), (1,)), ((), ()))
 
     stats_in[rank] = stats[rank]
@@ -520,13 +545,13 @@
     other_merged = merged_in.at[pl.ds(0, ny * nz - 1)]
     drain(other_merged, merged_sem.at[1])
 
-    by_seq = jnp.zeros((1, LANES), jnp.float32)
+    totals = jnp.zeros((1, 2 * LANES), jnp.float32)
     squares = jnp.zeros((1, LANES), jnp.float32)
     for slot in range(pack):
         log_norm = merge(merged_in, slot)
         picked = jnp.sum(merged_in[:, pack + slot, :], axis=0, keepdims=True)
         gain = jnp.where(filled, picked - log_norm, 0.0)
-        by_seq = by_seq + lax.dot_general(
+        totals = totals + lax.dot_general(
             jnp.broadcast_to(gain, (8, LANES)),
             insides[slot],
             contract,
@@ -535,7 +560,8 @@
         )[0:1, :]
         squares = squares + jnp.where(filled, log_norm * log_norm, 0.0)
     squares = jnp.sum(squares, axis=1, keepdims=True)
-    sums[...] = jnp.where(lane == seqs, squares, by_seq)
+    sums[0:1, :] = jnp.where(lane == seqs, squares, totals[:, :LANES])
+    sums[1:2, :] = totals[:, LANES:]
     sums_in[rank] = sums[...]
     for dx in sorted(range(nx), key=lambda d: -far(d, nx)):
         for dc in (0, 1):
@@ -550,15 +576,6 @@
                 device_id=(y, tx, twin if dc else core, z),
                 device_id_type=MESH,
             ).start()
-    pair_ids = iota((LANES, LANES), 0)
-    select = jnp.zeros((LANES, LANES), jnp.float32)
-    seq_ids = iota((LANES, LANES), 1)
-    margins = jnp.zeros((1, LANES), jnp.float32)
-    for p in range(pairs):
-        hit = jnp.where(seq_ids == pairs_ref[2 * p], 1.0, 0.0)
-        hit = hit - jnp.where(seq_ids == pairs_ref[2 * p + 1], 1.0, 0.0)
-        select = jnp.where(pair_ids == p, hit, select)
-        margins = jnp.where(lane == p, margins_ref[p], margins)
     live = functools.reduce(jnp.add, lens).astype(jnp.float32)
 
     drain(others, parcel_sem.at[0])
@@ -570,19 +587,12 @@
     other_sums = sums_in.at[pl.ds(0, owners - 1)]
     drain(other_sums, sums_sem.at[1])
 
-    row = functools.reduce(jnp.add, [sums_in[k] for k in range(owners)])
-    seq_row = jnp.where(lane < seqs, row, 0.0)
-    difference = lax.dot_general(
-        jnp.broadcast_to(seq_row, (8, LANES)),
-        select,
-        contract,
-        precision=lax.Precision.HIGHEST,
-        preferred_element_type=jnp.float32,
-    )[0:1, :]
+    table = functools.reduce(jnp.add, [sums_in[k] for k in range(owners)])
+    row, difference = table[0:1, :], table[1:2, :]
     score = -pref_beta * (difference - margins)
     pair_row = jnp.maximum(score, 0.0) + log_one_plus(jnp.exp(-jnp.abs(score)))
     z_row = zloss_weight * row / live
-    out_ref[0:1, :] = seq_row
+    out_ref[0:1, :] = row
     out_ref[1:2, :] = pair_row
     out_ref[2:3, :] = z_row
     out_ref[3:8, :] = jnp.zeros((5, LANES), jnp.float32)
@@ -613,14 +623,14 @@
         out_shape=jax.ShapeDtypeStruct((8, LANES), f32),
         in_specs=[
             pl.BlockSpec(memory_space=pl.ANY),
-            pl.BlockSpec(memory_space=pl.ANY),
-            pl.BlockSpec(memory_space=vmem),
-            pl.BlockSpec(memory_space=pltpu.SMEM),
-            pl.BlockSpec(memory_space=pltpu.SMEM),
-            pl.BlockSpec(memory_space=pltpu.SMEM),
-        ],
+        ]
+        * 6,
         out_specs=pl.BlockSpec(memory_space=vmem),
         scratch_shapes=[
+            vmem((1, window), i32),
+            pltpu.SMEM((seqs,), i32),
+            pltpu.SMEM((seqs,), i32),
+            pltpu.SMEM((seqs // 2,), f32),
             vmem((window, width), bf16),
             vmem((width, columns), bf16),
             vmem((2 * plane, slots, LANES), bf16),
@@ -635,9 +645,9 @@
             vmem((2 * nx, 4, LANES), f32),
             vmem((4, LANES), f32),
             vmem((ny * nz, 4, LANES), f32),
-            vmem((1, LANES), f32),
-            vmem((2 * nx, 1, LANES), f32),
-            dma((2,)),
+            vmem((2, LANES), f32),
+            vmem((2 * nx, 2, LANES), f32),
+            dma((6,)),
             dma((2,)),
             dma((2,)),
             dma(()),

time: 70.4 us -> 69.7 us (0.990)
  no operation moved by 1% of the time
where the time goes in v5:
time: 69.7 us; the launch traced here: 69.6 us
  Pallas kernels  69 us (99%)
    pallas_call x1, Pallas kernels, per_device(): pl.pallas_call(functools.partial(kernel, dims), out_shape=jax.ShapeDtypeS...  67.7 us

profile of v5, /device:TPU:1, one launch (start us, length us, event | category | flops | bytes accessed | tf_op | source)
XLA Modules:
  0.0 69.6 jit_solution(7806485438058574955)
XLA Ops:
  0.6 67.7 %shard_map.85.results_ref = f32[8,128]{1,0:T(8,128)} custom-call(bf16[120,4096]{1,0:T(8,128)(2,1)} %hidden_hbm.1, bf16[4096,384]{1,0:T(8,128)(2,1)} %weight_hbm.1, s32[1,120]{1,0:T(1,128)} %bitcast.4, s32[32]{0:T(128)} %lengths_hbm.1, s32[32]{0:T(128)} %pairs_hbm.1, f32[16]{0:T(128)} %margins_hbm.1), custom_call_target="tpu_custom_call" | custom-call | tf_op jit(solution)/shard_map/pallas_call | solution.py:621
  68.4 1.3 %shard_map.86 = (f32[1,32]{1,0:T(1,128)}, f32[1,16]{1,0:T(1,128)}, f32[1,1]{1,0:T(1,128)}) custom-call(f32[8,128]{1,0:T(8,128)} %shard_map.85.results_ref), custom_call_target="tpu_custom_call" | custom-call | tf_op jit(solution)/shard_map/pallas_call | solution.py:663

commit v6 on v5

--- a/solution.py
+++ b/solution.py
@@ -258,6 +258,28 @@
         cy, cx, cz = shifted(-node[0] + ny, -node[1] + nx, -node[2] + nz)
         return (cy * nx + cx) * nz + cz
 
+    far = lambda n, size: min(n, size - n)
+    plane_steps = sorted(
+        [(a, b) for a in range(ny) for b in range(nx)],
+        key=lambda s: -(far(s[0], ny) + far(s[1], nx)),
+    )
+    plane_peers = [(a, b, c) for a, b in plane_steps for c in (0, 1) if (a, b, c) != (0, 0, 0)]
+
+    def peer_of(step):
+        py, px, _ = shifted(step[0], step[1], 0)
+        pc = twin if step[2] else core
+        return py, px, pc
+
+    barrier = pltpu.get_barrier_semaphore()
+    for step in plane_peers:
+        py, px, pc = peer_of(step)
+        pl.semaphore_signal(barrier, inc=1, device_id=(py, px, pc, z), device_id_type=MESH)
+    z_steps = sorted({1 % nz, nz - 1} - {0})
+    for dz in z_steps:
+        pl.semaphore_signal(
+            barrier, inc=1, device_id=(y, x, core, (z + dz) % nz), device_id_type=MESH
+        )
+
     load_hidden = pltpu.make_async_copy(hidden_hbm, hidden, load_sem.at[0])
     load_weight = pltpu.make_async_copy(weight_hbm, weight, load_sem.at[1])
     load_hidden.start()
@@ -269,28 +291,6 @@
     ]
     for copy in load_small:
         copy.start()
-
-    far = lambda n, size: min(n, size - n)
-    plane_steps = sorted(
-        [(a, b) for a in range(ny) for b in range(nx)],
-        key=lambda s: -(far(s[0], ny) + far(s[1], nx)),
-    )
-    plane_peers = [(a, b, c) for a, b in plane_steps for c in (0, 1) if (a, b, c) != (0, 0, 0)]
-
-    def peer_of(step):
-        py, px, _ = shifted(step[0], step[1], 0)
-        pc = twin if step[2] else core
-        return py, px, pc
-
-    barrier = pltpu.get_barrier_semaphore()
-    for step in plane_peers:
-        py, px, pc = peer_of(step)
-        pl.semaphore_signal(barrier, inc=1, device_id=(py, px, pc, z), device_id_type=MESH)
-    z_steps = sorted({1 % nz, nz - 1} - {0})
-    for dz in z_steps:
-        pl.semaphore_signal(
-            barrier, inc=1, device_id=(y, x, core, (z + dz) % nz), device_id_type=MESH
-        )
 
     for copy in load_small:
         copy.wait()

time: 69.7 us -> 69.7 us (level)
  no operation moved by 1% of the time
where the time goes in v6:
time: 69.7 us; the launch traced here: 69.6 us
  Pallas kernels  69 us (99%)
    pallas_call x1, Pallas kernels, per_device(): pl.pallas_call(functools.partial(kernel, dims), out_shape=jax.ShapeDtypeS...  67.7 us

profile of v6, /device:TPU:1, one launch (start us, length us, event | category | flops | bytes accessed | tf_op | source)
XLA Modules:
  0.0 69.6 jit_solution(13239303632482241845)
XLA Ops:
  0.6 67.7 %shard_map.85.results_ref = f32[8,128]{1,0:T(8,128)} custom-call(bf16[120,4096]{1,0:T(8,128)(2,1)} %hidden_hbm.1, bf16[4096,384]{1,0:T(8,128)(2,1)} %weight_hbm.1, s32[1,120]{1,0:T(1,128)} %bitcast.4, s32[32]{0:T(128)} %lengths_hbm.1, s32[32]{0:T(128)} %pairs_hbm.1, f32[16]{0:T(128)} %margins_hbm.1), custom_call_target="tpu_custom_call" | custom-call | tf_op jit(solution)/shard_map/pallas_call | solution.py:621
  68.4 1.3 %shard_map.86 = (f32[1,32]{1,0:T(1,128)}, f32[1,16]{1,0:T(1,128)}, f32[1,1]{1,0:T(1,128)}) custom-call(f32[8,128]{1,0:T(8,128)} %shard_map.85.results_ref), custom_call_target="tpu_custom_call" | custom-call | tf_op jit(solution)/shard_map/pallas_call | solution.py:663
